TPU v7x, 32 devices: a whole 2x2x4 slice. The times are simulated.
32 devices in a mesh: member: 2 (over x), graph: 8 (over z, y), chan: 2 (over core).
Axes of the slice: x: 2, y: 2, z: 4, core: 2. Of those that a mesh axis runs over, the one named last changes fastest.
Arguments:
- grid_state: bfloat16 [16384, 256], P(('member', 'graph')), parts along dimension 0, may hold values from -6 to 6
- w_src: bfloat16 [256, 512], P(None, 'chan'), may hold values from -0.375 to 0.375
- bias_src: float32 [512], P('chan'), may hold values from -3 to 3
- mesh_embed: bfloat16 [5120, 512], P('graph', 'chan'), may hold values from -6 to 6
- w_node: bfloat16 [512, 512], P('chan'), may hold values from -0.25 to 0.25
- w_dec: bfloat16 [512, 256], P('chan'), may hold values from -0.125 to 0.125
- slot_src: int32 [8, 8, 1024], P('graph'), may hold values from 0 to 1023, as said below
- slot_dst: int32 [8, 8, 1024], P(None, 'graph'), may hold values from 0 to 639, as said below
- slot_count: int32 [8, 8], replicated, may hold values from 1 to 1024, as said below
Outputs:
- grid_out: bfloat16 [16384, 256], P(('member', 'graph'), 'chan'), parts along dimension 0
There are 2 independent parts, one for each index of `member`. A program takes and returns all parts, laid end to end along the dimension named above; an argument that names none is the same for every part. Nothing has to cross between parts.
Inputs may be any that keep to these rules, and one draw needn't show every extreme that they name: `slot_src`: slots at or past the live count hold arbitrary values in the same range. `slot_dst`: slots at or past the live count hold arbitrary values in the same range. slot_count[s, d] counts the live leading slots of the 1024 from shard s to shard d; in every draw some receiving shard has all 1024 slots live from every sender.
All inputs are finite; a program needn't handle non-finite values.
Results may differ from a plain program's by a relative error of at most 0.0056.
Values may be sent and summed in bfloat16 or wider, within the bound.
A program may use at most 64 MiB of HBM per device.

v0:
```python
import functools
import math

import jax
import jax.numpy as jnp
from jax import lax
from jax.experimental import pallas as pl
from jax.experimental.pallas import tpu as pltpu
from jax.sharding import PartitionSpec as P

CHUNKS = 4
HOT = jnp.float8_e4m3fn
VMEM_BUDGET = 48 * 2**20
MESH = pl.DeviceIdType.MESH
NT = (((1,), (1,)), ((), ()))


def edge_network(source_rows, w_src, bias_src):
    return jax.nn.silu(
        jnp.dot(source_rows, w_src, preferred_element_type=jnp.float32) + bias_src
    ).astype(jnp.bfloat16)


def segment_rows(values, indices, usable, row_count):
    slot_total = values.shape[0]
    width = values.shape[1]
    block_len = math.gcd(slot_total, 2048)
    block_count = slot_total // block_len
    targets = jnp.where(usable, indices, -1).reshape(block_count, block_len)
    pieces = values.reshape(block_count, block_len, width)
    row_ids = jnp.arange(row_count, dtype=jnp.int32)

    def add_block(summed, scan_item):
        row_target, piece_vals = scan_item
        one_hot = (row_ids[:, None] == row_target[None, :]).astype(jnp.bfloat16)
        return (summed + jnp.dot(one_hot, piece_vals, preferred_element_type=jnp.float32), None)

    result, unused = lax.scan(
        add_block, jnp.zeros((row_count, width), jnp.float32), (targets, pieces)
    )
    return result


def on_device(
    grid_state, w_src, bias_src, mesh_embed, w_node, w_dec, slot_src, slot_dst, slot_count
):
    peers = lax.axis_size("graph")
    own_index = lax.axis_index("graph")
    core_index = lax.axis_index("chan")
    capacity = slot_src.shape[2]
    positions = jnp.arange(capacity, dtype=jnp.int32)
    grid_rows = grid_state.shape[0]
    mesh_rows = mesh_embed.shape[0]
    sent_counts = lax.dynamic_slice_in_dim(slot_count, own_index, 1, 0)[0]
    recv_counts = lax.dynamic_slice_in_dim(slot_count, own_index, 1, 1)[:, 0]
    half_slots = capacity // 2
    chosen = lax.dynamic_slice_in_dim(slot_src[0], core_index * half_slots, half_slots, 1)
    picked = jnp.take(grid_state, chosen.reshape(-1), axis=0).reshape(
        peers, half_slots, grid_state.shape[1]
    )
    arrived = lax.all_to_all(picked, "graph", split_axis=0, concat_axis=0, tiled=True)
    joined = lax.all_gather(arrived, "chan", axis=1, tiled=True)
    messages = edge_network(joined.reshape(peers * capacity, grid_state.shape[1]), w_src, bias_src)
    arrive_ok = (positions[None, :] < recv_counts[:, None]).reshape(-1)
    dst_rows = slot_dst[:, 0, :].reshape(-1)
    aggregate = segment_rows(messages, dst_rows, arrive_ok, mesh_rows)
    partial_hidden = jnp.dot(
        aggregate.astype(jnp.bfloat16), w_node, preferred_element_type=jnp.float32
    )
    hidden_pre = lax.psum_scatter(partial_hidden, "chan", scatter_dimension=1, tiled=True)
    latent = (mesh_embed.astype(jnp.float32) + jax.nn.silu(hidden_pre)).astype(jnp.bfloat16)
    partial_proj = jnp.dot(latent, w_dec, preferred_element_type=jnp.float32)
    projected = lax.psum_scatter(partial_proj, "chan", scatter_dimension=1, tiled=True).astype(
        jnp.bfloat16
    )
    returned = jnp.take(projected, dst_rows, axis=0).reshape(peers, capacity, projected.shape[1])
    came_back = lax.all_to_all(returned, "graph", split_axis=0, concat_axis=0, tiled=True).reshape(
        peers * capacity, projected.shape[1]
    )
    send_ok = (positions[None, :] < sent_counts[:, None]).reshape(-1)
    decoded = segment_rows(came_back, slot_src[0].reshape(-1), send_ok, grid_rows)
    width_half = decoded.shape[1]
    own_cols = lax.dynamic_slice_in_dim(grid_state, core_index * width_half, width_half, 1)
    return (own_cols.astype(jnp.float32) + decoded).astype(jnp.bfloat16)


def silu(v):
    half = 0.5 * v
    return half + half * jnp.tanh(half)


def one_hot(first, rows, indices):
    row_ids = lax.broadcasted_iota(jnp.int32, (rows, indices.shape[1]), 0) + first
    return jnp.where(row_ids == indices, 1.0, 0.0).astype(HOT)


def graph_kernel(
    peers,
    x_ref, w_src_ref, bias_ref, embed_ref, w_node_ref, w_dec_ref, src_ref, dst_ref, count_ref,
    out_ref,
    x_all, src_own, src_in, dst_in, w_src_all, bias_all, embed_all, w_node_all, w_dec_all,
    enc, dec, hot, agg, proj, proj_all,
    local_sem, par_send, par_recv, idx_send, idx_recv,
    xo_send, xz_send, xy_send, x_recv, xm_send, xm_recv,
    po_send, pz_send, py_send, p_recv, pm_send, pm_recv, dec_send, dec_recv,
):
    lines = peers // 2
    me = lax.axis_index("graph")
    core = lax.axis_index("chan")
    mate = 1 - core
    line, side = me // 2, me % 2
    other = line * 2 + (1 - side)
    grid_rows, chans = x_ref.shape
    half_grid = grid_rows // 2
    piece = half_grid // CHUNKS
    mesh_rows = embed_ref.shape[0]
    half_mesh = mesh_rows // 2
    cols = chans // 2
    tile = enc.shape[3]
    tiles = grid_rows // tile
    capacity = src_ref.shape[2]

    def remote(src, dst, send, recv, graph, chan):
        return pltpu.make_async_remote_copy(
            src_ref=src, dst_ref=dst, send_sem=send, recv_sem=recv,
            device_id={"graph": graph, "chan": chan}, device_id_type=MESH,
        )

    barrier = pltpu.get_barrier_semaphore()
    for step in range(peers):
        for chan in range(2):
            if step == 0 and chan == 0:
                continue
            pl.semaphore_signal(
                barrier, inc=1,
                device_id={"graph": (me + step) % peers, "chan": (core + chan) % 2},
                device_id_type=MESH,
            )
    slots = lax.broadcasted_iota(jnp.int32, (1, capacity), 1)
    for to in range(peers):
        src_own[to] = jnp.where(slots < count_ref[me, to], src_ref[0, to : to + 1, :], -1)
    my_rows = pl.ds(pl.multiple_of(core * half_mesh, half_mesh), half_mesh)
    mate_rows = pl.ds(pl.multiple_of(mate * half_mesh, half_mesh), half_mesh)
    locals_ = [
        pltpu.make_async_copy(x_ref, x_all.at[me], local_sem.at[0]),
        pltpu.make_async_copy(w_src_ref, w_src_all.at[core], local_sem.at[1]),
        pltpu.make_async_copy(bias_ref, bias_all.at[core], local_sem.at[2]),
        pltpu.make_async_copy(embed_ref.at[my_rows], embed_all.at[core], local_sem.at[3]),
        pltpu.make_async_copy(w_node_ref, w_node_all.at[core], local_sem.at[4]),
        pltpu.make_async_copy(w_dec_ref, w_dec_all.at[core], local_sem.at[5]),
        pltpu.make_async_copy(src_own.at[me], src_in.at[me], local_sem.at[6]),
        pltpu.make_async_copy(dst_ref.at[me], dst_in.at[me], local_sem.at[7]),
    ]
    for copy in locals_:
        copy.start()
    for copy in locals_:
        copy.wait()
    pl.semaphore_wait(barrier, 2 * peers - 1)

    sends = []
    idx_copies = []
    for step in range(1, peers):
        to = (me + step) % peers
        for at, (ref, into) in enumerate(((src_own, src_in), (dst_ref, dst_in))):
            copy = remote(
                ref.at[to], into.at[me], idx_send.at[at, step], idx_recv.at[at, step], to, core
            )
            copy.start()
            idx_copies.append(copy)

    def nearest(at):
        return sorted((p for p in range(lines) if p != at), key=lambda p: (abs(p - at), p))

    from_line = [
        sum(jnp.where(line == at, nearest(at)[i], 0) for at in range(lines))
        for i in range(lines - 1)
    ]
    up, down = (line + 1) * 2 + side, (line - 1) * 2 + side

    def along(source, make):
        for going, target in (
            ((source <= line) & (line < lines - 1), up),
            ((source >= line) & (line > 0), down),
        ):
            @pl.when(going)
            def _(target=target):
                make(target).start()
            sends.append((going, functools.partial(make, target)))

    def begin(copy):
        copy.start()
        sends.append((None, lambda: copy))

    def x_part(shard, half, c):
        first = pl.multiple_of(half * half_grid, half_grid) + c * piece
        return x_all.at[shard, pl.ds(pl.multiple_of(first, piece), piece)]

    def x_own(c):
        first = pl.multiple_of(core * half_grid, half_grid) + c * piece
        return x_all.at[me, pl.ds(pl.multiple_of(first, piece), piece)]

    for c in range(CHUNKS):
        begin(remote(x_own(c), x_part(me, core, c), xy_send.at[line, c], x_recv.at[1, line, c], other, core))
        for at, (going, target) in enumerate(((line < lines - 1, up), (line > 0, down))):
            def make(c=c, at=at, target=target):
                return remote(
                    x_own(c), x_part(me, core, c), xo_send.at[at, c], x_recv.at[0, line, c],
                    target, core,
                )
            @pl.when(going)
            def _(make=make):
                make().start()
            sends.append((going, make))

    par_copies = [
        remote(w_src_all.at[core], w_src_all.at[core], par_send.at[0], par_recv.at[0], me, mate),
        remote(bias_all.at[core], bias_all.at[core], par_send.at[1], par_recv.at[1], me, mate),
        remote(embed_ref.at[mate_rows], embed_all.at[core], par_send.at[2], par_recv.at[2], me, mate),
        remote(w_node_all.at[core], w_node_all.at[core], par_send.at[3], par_recv.at[3], me, mate),
        remote(w_dec_all.at[core], w_dec_all.at[core], par_send.at[4], par_recv.at[4], me, mate),
    ]
    for copy in par_copies:
        copy.start()

    def to_mate(flip, source, c, shard):
        ref = x_part(shard, core, c)
        begin(remote(ref, ref, xm_send.at[flip, source, c], xm_recv.at[flip, source, c], me, mate))

    def relay(i, c):
        source = from_line[i]
        shard = source * 2 + side
        ref = x_part(shard, core, c)
        remote(ref, ref, xz_send.at[source, c], x_recv.at[0, source, c], me, mate).wait_recv()
        along(source, lambda target: remote(
            ref, ref, xz_send.at[source, c], x_recv.at[0, source, c], target, core))
        begin(remote(ref, ref, xy_send.at[source, c], x_recv.at[1, source, c], other, core))
        to_mate(0, source, c, shard)

    def take(source, c):
        shard = source * 2 + (1 - side)
        ref = x_part(shard, core, c)
        remote(ref, ref, xz_send.at[source, c], x_recv.at[1, source, c], me, mate).wait_recv()
        to_mate(1, source, c, shard)

    def build_enc(i, carry):
        shard = (me + i) % peers
        hot[: half_mesh, :] = one_hot(core * half_mesh, half_mesh, dst_ref[shard])
        for t in range(tiles):
            picks = one_hot(t * tile, tile, src_in[shard])
            enc[shard, t] = lax.dot_general(
                hot[: half_mesh, :], picks, NT, preferred_element_type=jnp.float32
            ).astype(jnp.bfloat16)
        return carry

    def build_dec(i, carry):
        shard = (me + i) % peers
        hot[...] = one_hot(0, mesh_rows, dst_in[shard])
        for t in range(half_grid // 256):
            first = pl.multiple_of(core * half_grid, half_grid) + t * 256
            picks = one_hot(first, 256, src_own[shard])
            dec[shard, pl.ds(pl.multiple_of(first, 256), 256), :] = lax.dot_general(
                picks, hot[...], NT, preferred_element_type=jnp.float32
            ).astype(jnp.bfloat16)
        return carry

    done = {build_enc: 0, build_dec: 0}
    pending = []

    def dec_copy(i, half):
        shard = (me + i) % peers
        ref = dec.at[shard, pl.ds(pl.multiple_of(half * half_grid, half_grid), half_grid)]
        return remote(ref, ref, dec_send.at[shard], dec_recv.at[shard], me, mate)

    def flush():
        while pending:
            begin(dec_copy(pending.pop(0), core))

    def build(which, count):
        first = done[which]
        last = min(first + count, peers)
        if last > first:
            flush()
            lax.fori_loop(first, last, which, 0)
            if which is build_dec:
                pending.extend(range(first, last))
        done[which] = last

    def encode(shard):
        def step(t, carry):
            rows = pl.ds(pl.multiple_of(t * tile, tile), tile)
            for h in range(2):
                pre = jnp.dot(
                    x_all[shard, rows, :], w_src_all[h], preferred_element_type=jnp.float32
                ) + bias_all[h]
                agg[h] += jnp.dot(
                    enc[shard, t], silu(pre).astype(jnp.bfloat16),
                    preferred_element_type=jnp.float32,
                )
            return carry
        lax.fori_loop(0, tiles, step, 0)

    def encode_from(flip, source):
        shard = source * 2 + (side if flip == 0 else 1 - side)
        for c in range(CHUNKS):
            ref = x_part(shard, mate, c)
            remote(ref, ref, xm_send.at[flip, source, c], xm_recv.at[flip, source, c], me, mate).wait_recv()
        encode(shard)

    agg[...] = jnp.zeros_like(agg)
    out_ref[...] = x_all[me, :, pl.ds(pl.multiple_of(core * cols, cols), cols)].astype(jnp.float32)
    build(build_enc, 1)
    build(build_dec, 1)
    for copy in par_copies:
        copy.wait()
    encode(me)
    for copy in idx_copies:
        copy.wait()
    flush()
    build(build_enc, peers // 4)
    last = lines - 2
    for i in range(lines - 1):
        for c in range(CHUNKS):
            relay(i, c)
            if i == 0:
                build(build_enc, peers // CHUNKS // 4)
            else:
                take(from_line[i - 1], c)
                if c < CHUNKS - 1:
                    build(build_dec, 1)
        if i == 0:
            for c in range(CHUNKS):
                take(line, c)
            build(build_enc, peers)
        elif i == 1:
            encode_from(0, from_line[0])
            encode_from(1, line)
            build(build_dec, 1)
        else:
            encode_from(0, from_line[i - 1])
            encode_from(1, from_line[i - 2])
            build(build_dec, 1)
    encode_from(0, from_line[last])
    take(from_line[last], 0)
    encode_from(1, from_line[last - 1])
    for c in range(1, CHUNKS):
        take(from_line[last], c)
    encode_from(1, from_line[last])

    hidden = sum(
        jnp.dot(agg[h].astype(jnp.bfloat16), w_node_all[h], preferred_element_type=jnp.float32)
        for h in range(2)
    )
    width = hidden.shape[1] // 2
    projected = sum(
        jnp.dot(
            (
                embed_all[h].astype(jnp.float32) + silu(hidden[:, h * width : (h + 1) * width])
            ).astype(jnp.bfloat16),
            w_dec_all[h], preferred_element_type=jnp.float32,
        )
        for h in range(2)
    ).astype(jnp.bfloat16)
    for h in range(2):
        proj[h] = projected[:, h * cols : (h + 1) * cols]

    own_copy = pltpu.make_async_copy(proj.at[core], proj_all.at[me, my_rows], local_sem.at[0])
    own_copy.start()
    into = proj_all.at[me, my_rows]
    for flip in range(2):
        chan = (core + flip) % 2
        begin(remote(proj.at[chan], into, py_send.at[line, flip], p_recv.at[1, line, core], other, chan))
        for at, (going, target) in enumerate(((line < lines - 1, up), (line > 0, down))):
            def make(flip=flip, chan=chan, at=at, target=target):
                return remote(
                    proj.at[chan], into, po_send.at[at, flip], p_recv.at[0, line, core],
                    target, chan,
                )
            @pl.when(going)
            def _(make=make):
                make().start()
            sends.append((going, make))
    begin(remote(proj.at[mate], into, pm_send.at[0], pm_recv.at[0], me, mate))

    def p_part(shard, half):
        return proj_all.at[shard, pl.ds(pl.multiple_of(half * half_mesh, half_mesh), half_mesh)]

    def p_wait(flip, source, half):
        ref = p_part(source * 2 + (side if flip == 0 else 1 - side), half)
        remote(ref, ref, pz_send.at[source, half], p_recv.at[flip, source, half], me, mate).wait_recv()

    def p_relay(i):
        source = from_line[i]
        for half in (core, mate):
            p_wait(0, source, half)
            ref = p_part(source * 2 + side, half)
            along(source, lambda target, half=half, ref=ref: remote(
                ref, ref, pz_send.at[source, half], p_recv.at[0, source, half], target, core))
            begin(remote(ref, ref, py_send.at[source, half], p_recv.at[1, source, half], other, core))

    def decode(shard):
        def step(t, carry):
            rows = pl.ds(pl.multiple_of(t * half_grid, half_grid), half_grid)
            out_ref[rows, :] += jnp.dot(
                dec[shard, rows, :], proj_all[shard], preferred_element_type=jnp.float32
            )
            return carry
        lax.fori_loop(0, 2, step, 0)

    flush()
    left = peers - done[build_dec]
    for i in range(lines - 1):
        build(build_dec, -(-left // (lines - 1)))
        p_relay(i)
    flush()
    for i in range(peers):
        dec_copy(i, mate).wait_recv()
    own_copy.wait()
    remote(proj.at[mate], into, pm_send.at[0], pm_recv.at[0], me, mate).wait_recv()
    decode(me)
    for i in range(lines - 1):
        decode(from_line[i] * 2 + side)
    for source in [line] + from_line:
        for half in (core, mate):
            p_wait(1, source, half)
        decode(source * 2 + 1 - side)

    for going, make in sends:
        if going is None:
            make().wait_send()
        else:
            @pl.when(going)
            def _(make=make):
                make().wait_send()


def fused(grid_state, w_src, bias_src, mesh_embed, w_node, w_dec, slot_src, slot_dst, slot_count):
    peers = lax.axis_size("graph")
    capacity = slot_src.shape[2]
    grid_rows, chans = grid_state.shape
    mesh_rows = mesh_embed.shape[0]
    hidden = w_src.shape[1]
    lines = peers // 2
    bf16, f32 = jnp.bfloat16, jnp.float32
    dma = pltpu.SemaphoreType.DMA
    vmem = pl.BlockSpec(memory_space=pltpu.VMEM)
    tile = grid_rows // 2
    return pl.pallas_call(
        functools.partial(graph_kernel, peers),
        out_shape=jax.ShapeDtypeStruct((grid_rows, chans // 2), f32),
        in_specs=[pl.BlockSpec(memory_space=pl.ANY)] * 6 + [vmem] * 2 + [pl.BlockSpec(memory_space=pltpu.SMEM)],
        out_specs=vmem,
        scratch_shapes=[
            pltpu.VMEM((peers, grid_rows, chans), bf16),
            pltpu.VMEM((peers, 1, capacity), jnp.int32),
            pltpu.VMEM((peers, 1, capacity), jnp.int32),
            pltpu.VMEM((peers, 1, capacity), jnp.int32),
            pltpu.VMEM((2,) + w_src.shape, bf16),
            pltpu.VMEM((2, 1, hidden), f32),
            pltpu.VMEM((2, mesh_rows // 2, hidden), bf16),
            pltpu.VMEM((2,) + w_node.shape, bf16),
            pltpu.VMEM((2,) + w_dec.shape, bf16),
            pltpu.VMEM((peers, grid_rows // tile, mesh_rows // 2, tile), bf16),
            pltpu.VMEM((peers, grid_rows, mesh_rows), bf16),
            pltpu.VMEM((mesh_rows, capacity), HOT),
            pltpu.VMEM((2, mesh_rows // 2, hidden), f32),
            pltpu.VMEM((2, mesh_rows // 2, chans // 2), bf16),
            pltpu.VMEM((peers, mesh_rows, chans // 2), bf16),
            dma((8,)), dma((5,)), dma((5,)), dma((2, peers)), dma((2, peers)),
            dma((2, CHUNKS)), dma((lines, CHUNKS)), dma((lines, CHUNKS)), dma((2, lines, CHUNKS)),
            dma((2, lines, CHUNKS)), dma((2, lines, CHUNKS)),
            dma((2, 2)), dma((lines, 2)), dma((lines, 2)), dma((2, lines, 2)), dma((1,)), dma((1,)), dma((peers,)), dma((peers,)),
        ],
        compiler_params=pltpu.CompilerParams(collective_id=0, has_side_effects=True),
    )(grid_state, w_src, bias_src[None, :], mesh_embed, w_node, w_dec, slot_src, slot_dst, slot_count).astype(bf16)


def held_bytes(peers, grid_state, mesh_embed, *rest):
    grid_rows, chans = grid_state.shape
    mesh_rows = mesh_embed.shape[0]
    return 2 * peers * grid_rows * (chans + 2 * mesh_rows)


def per_device(grid_state, w_src, bias_src, mesh_embed, *rest):
    peers = lax.axis_size("graph")
    fits = (
        peers % 2 == 0
        and peers >= 4
        and lax.axis_size("chan") == 2
        and held_bytes(peers, grid_state, mesh_embed) <= VMEM_BUDGET
    )
    body = fused if fits else on_device
    return body(grid_state, w_src, bias_src, mesh_embed, *rest)


def solution(mesh):
    placed = (
        P(("member", "graph"), None),
        P(None, "chan"),
        P("chan"),
        P("graph", "chan"),
        P("chan", None),
        P("chan", None),
        P("graph", None, None),
        P(None, "graph", None),
        P(),
    )
    return jax.shard_map(
        per_device,
        mesh=mesh,
        in_specs=placed,
        out_specs=P(("member", "graph"), "chan"),
        check_vma=False,
    )
```

profile of v0, /device:TPU:0, one launch (start us, length us, event | category | flops | bytes accessed | tf_op | source)
XLA Modules:
  0.0 66.4 jit_solution(10397433791934457494)
XLA Ops:
  0.0 64.7 %shard_map.91 = f32[1024,128]{1,0:T(8,128)} custom-call(bf16[1024,256]{1,0:T(8,128)(2,1)} %x_ref.1, bf16[256,256]{1,0:T(8,128)(2,1)} %w_src_ref.1, f32[1,256]{1,0:T(1,128)} %bitcast.1, bf16[640,256]{1,0:T(8,128)(2,1)} %embed_ref.1, bf16[256,512]{1,0:T(8,128)(2,1)} %w_node_ref.1, bf16[256,256]{1,0:T(8,128)(2,1)} %w_dec_ref.1, s32[1,8,1024]{2,1,0:T(8,128)} %src_ref.1, ...), custom_call_target="tpu_custom_call" | custom-call | tf_op jit(solution)/shard_map/pallas_call | solution.py:447
  64.7 1.8 %convert_element_type.3 = bf16[1024,128]{1,0:T(8,128)(2,1)} convert(f32[1024,128]{1,0:T(8,128)} %shard_map.91) | non-fusion elementwise | flops 131072 | bytes 786432 | tf_op jit(solution)/shard_map/convert_element_type | solution.py:474
where the time goes:
time: 66.7 us; the launch traced here: 66.4 us
  Pallas kernels  64.7 us (97%)
  other arithmetic  1.77 us (3%)
    pallas_call x1, Pallas kernels, fused(): pl.pallas_call(functools.partial(graph_kernel, peers), out_shape=jax.Shap...  64.7 us
    convert_element_type x1, other arithmetic, fused(): return pl.pallas_call(functools.partial(graph_kernel, peers), out_shape=j...  1.77 us

commit v1 on v0

v1 whole, which is shorter than its diff:
```python
import functools
import math

import jax
import jax.numpy as jnp
from jax import lax
from jax.experimental import pallas as pl
from jax.experimental.pallas import tpu as pltpu
from jax.sharding import PartitionSpec as P

CHUNKS = 4
SUBS = 2
HOT = jnp.float8_e4m3fn
VMEM_BUDGET = 48 * 2**20
MESH = pl.DeviceIdType.MESH
NT = (((1,), (1,)), ((), ()))


def edge_network(source_rows, w_src, bias_src):
    return jax.nn.silu(
        jnp.dot(source_rows, w_src, preferred_element_type=jnp.float32) + bias_src
    ).astype(jnp.bfloat16)


def segment_rows(values, indices, usable, row_count):
    slot_total = values.shape[0]
    width = values.shape[1]
    block_len = math.gcd(slot_total, 2048)
    block_count = slot_total // block_len
    targets = jnp.where(usable, indices, -1).reshape(block_count, block_len)
    pieces = values.reshape(block_count, block_len, width)
    row_ids = jnp.arange(row_count, dtype=jnp.int32)

    def add_block(summed, scan_item):
        row_target, piece_vals = scan_item
        one_hot = (row_ids[:, None] == row_target[None, :]).astype(jnp.bfloat16)
        return (summed + jnp.dot(one_hot, piece_vals, preferred_element_type=jnp.float32), None)

    result, unused = lax.scan(
        add_block, jnp.zeros((row_count, width), jnp.float32), (targets, pieces)
    )
    return result


def on_device(
    grid_state, w_src, bias_src, mesh_embed, w_node, w_dec, slot_src, slot_dst, slot_count
):
    peers = lax.axis_size("graph")
    own_index = lax.axis_index("graph")
    core_index = lax.axis_index("chan")
    capacity = slot_src.shape[2]
    positions = jnp.arange(capacity, dtype=jnp.int32)
    grid_rows = grid_state.shape[0]
    mesh_rows = mesh_embed.shape[0]
    sent_counts = lax.dynamic_slice_in_dim(slot_count, own_index, 1, 0)[0]
    recv_counts = lax.dynamic_slice_in_dim(slot_count, own_index, 1, 1)[:, 0]
    half_slots = capacity // 2
    chosen = lax.dynamic_slice_in_dim(slot_src[0], core_index * half_slots, half_slots, 1)
    picked = jnp.take(grid_state, chosen.reshape(-1), axis=0).reshape(
        peers, half_slots, grid_state.shape[1]
    )
    arrived = lax.all_to_all(picked, "graph", split_axis=0, concat_axis=0, tiled=True)
    joined = lax.all_gather(arrived, "chan", axis=1, tiled=True)
    messages = edge_network(joined.reshape(peers * capacity, grid_state.shape[1]), w_src, bias_src)
    arrive_ok = (positions[None, :] < recv_counts[:, None]).reshape(-1)
    dst_rows = slot_dst[:, 0, :].reshape(-1)
    aggregate = segment_rows(messages, dst_rows, arrive_ok, mesh_rows)
    partial_hidden = jnp.dot(
        aggregate.astype(jnp.bfloat16), w_node, preferred_element_type=jnp.float32
    )
    hidden_pre = lax.psum_scatter(partial_hidden, "chan", scatter_dimension=1, tiled=True)
    latent = (mesh_embed.astype(jnp.float32) + jax.nn.silu(hidden_pre)).astype(jnp.bfloat16)
    partial_proj = jnp.dot(latent, w_dec, preferred_element_type=jnp.float32)
    projected = lax.psum_scatter(partial_proj, "chan", scatter_dimension=1, tiled=True).astype(
        jnp.bfloat16
    )
    returned = jnp.take(projected, dst_rows, axis=0).reshape(peers, capacity, projected.shape[1])
    came_back = lax.all_to_all(returned, "graph", split_axis=0, concat_axis=0, tiled=True).reshape(
        peers * capacity, projected.shape[1]
    )
    send_ok = (positions[None, :] < sent_counts[:, None]).reshape(-1)
    decoded = segment_rows(came_back, slot_src[0].reshape(-1), send_ok, grid_rows)
    width_half = decoded.shape[1]
    own_cols = lax.dynamic_slice_in_dim(grid_state, core_index * width_half, width_half, 1)
    return (own_cols.astype(jnp.float32) + decoded).astype(jnp.bfloat16)


def silu(v):
    half = 0.5 * v
    return half + half * jnp.tanh(half)


def one_hot(first, rows, indices):
    row_ids = lax.broadcasted_iota(jnp.int32, (rows, indices.shape[1]), 0) + first
    return jnp.where(row_ids == indices, 1.0, 0.0).astype(HOT)


def inner_of(line, lines):
    return line + 1 if line < lines // 2 else line - 1


def outer_of(line, lines):
    return line - 1 if line < lines // 2 else line + 1


def arrival_order(line, lines):
    stages = [(0, 0, line, 1)]
    for source in range(lines):
        gap = abs(source - line)
        if gap:
            stages.append((gap - 1, gap, source, 0))
            stages.append((lines if source == inner_of(line, lines) else gap, gap, source, 1))
    return sorted(stages, key=lambda at: (at[0], at[3], at[1], at[2]))


def link_pieces(line, lines, pieces):
    inner, outer = inner_of(line, lines), outer_of(line, lines)

    def extra(to):
        return pieces if outer_of(to, lines) == line else pieces // 2 if inner_of(to, lines) == line else 0

    up = pieces * (line + 1) + extra(line + 1) if line < lines - 1 else 0
    down = pieces * (lines - line) + extra(line - 1) if line > 0 else 0
    across = pieces * lines - sum(
        pieces if p == outer else pieces - pieces // 2 if p == inner else 0 for p in range(lines) if p != line
    )
    return up, down, across


def graph_kernel(
    peers,
    x_ref, w_src_ref, bias_ref, embed_ref, w_node_ref, w_dec_ref, src_ref, dst_ref, count_ref,
    out_ref,
    x_all, idx_own, idx_in, src_vmem, dst_vmem, count_smem, w_src_all, bias_all, embed_all, w_node_all, w_dec_all,
    enc, dec, hot, msg, agg, acc, proj_mate, proj_all,
    ready, local_sem, par_send, par_recv, idx_send, idx_recv,
    x_send, xz_recv, xy_recv, xm_recv, p_send, pz_recv, py_recv, pm_recv, dec_send, dec_recv,
):
    lines = peers // 2
    me = lax.axis_index("graph")
    core = lax.axis_index("chan")
    mate = 1 - core
    line, side = me // 2, me % 2
    other = line * 2 + (1 - side)
    up, down = (line + 1) * 2 + side, (line - 1) * 2 + side
    has_up, has_down = line < lines - 1, line > 0
    low_half = line < lines // 2
    grid_rows, chans = x_ref.shape
    half_grid = grid_rows // 2
    block = half_grid // CHUNKS
    mesh_rows = embed_ref.shape[0]
    half_mesh = mesh_rows // 2
    part_mesh = half_mesh // SUBS
    cols = chans // 2
    capacity = src_ref.shape[2]
    UP, DOWN, ACROSS, MATE = range(4)

    def remote(src, dst, send, recv, graph, chan):
        return pltpu.make_async_remote_copy(
            src_ref=src, dst_ref=dst, send_sem=send, recv_sem=recv,
            device_id={"graph": graph, "chan": chan}, device_id_type=MESH,
        )

    def by_line(values):
        return sum(jnp.where(line == at, values[at], 0) for at in range(lines))

    inner = jnp.where(low_half, line + 1, line - 1)
    outer = jnp.where(low_half, line - 1, line + 1)
    barrier = pltpu.get_barrier_semaphore()

    def greet(graph, chan):
        pl.semaphore_signal(barrier, inc=1, device_id={"graph": graph, "chan": chan}, device_id_type=MESH)

    greet(me, mate)
    for chan in (core, mate):
        greet(other, chan)
        pl.when(has_up)(functools.partial(greet, up, chan))
        pl.when(has_down)(functools.partial(greet, down, chan))
    my_rows = pl.ds(pl.multiple_of(core * half_mesh, half_mesh), half_mesh)
    mate_rows = pl.ds(pl.multiple_of(mate * half_mesh, half_mesh), half_mesh)
    own_rows = pl.ds(pl.multiple_of(me * grid_rows, grid_rows), grid_rows)
    locals_ = [
        pltpu.make_async_copy(src_ref, src_vmem, local_sem.at[0]),
        pltpu.make_async_copy(dst_ref, dst_vmem, local_sem.at[1]),
        pltpu.make_async_copy(count_ref, count_smem, local_sem.at[2]),
        pltpu.make_async_copy(x_ref, x_all.at[own_rows], local_sem.at[3]),
        pltpu.make_async_copy(w_src_ref, w_src_all.at[core], local_sem.at[4]),
        pltpu.make_async_copy(bias_ref, bias_all.at[core], local_sem.at[5]),
        pltpu.make_async_copy(w_node_ref, w_node_all.at[core], local_sem.at[6]),
        pltpu.make_async_copy(w_dec_ref, w_dec_all.at[core], local_sem.at[7]),
        pltpu.make_async_copy(embed_ref.at[my_rows], embed_all.at[core], local_sem.at[8]),
    ]
    for copy in locals_:
        copy.start()
    for copy in locals_[:3]:
        copy.wait()
    slots = lax.broadcasted_iota(jnp.int32, (1, capacity), 1)
    for to in range(peers):
        idx_own[to, 0:1, :] = jnp.where(slots < count_smem[me, to], src_vmem[0, to : to + 1, :], -1)
        idx_own[to, 1:2, :] = dst_vmem[to]
    idx_in[me] = idx_own[me]
    for copy in locals_[3:]:
        copy.wait()
    pl.semaphore_wait(barrier, 3 + 2 * jnp.where(has_up, 1, 0) + 2 * jnp.where(has_down, 1, 0))

    def send_idx(to):
        remote(idx_own.at[to], idx_in.at[me], idx_send.at[0], idx_recv.at[me], to, core).start()

    def x_part(shard, c, half=core):
        first = shard * grid_rows + c * 2 * block + half * block
        return x_all.at[pl.ds(pl.multiple_of(first, block), block)]

    send_idx(other)
    pl.when(has_up)(functools.partial(send_idx, up))
    pl.when(has_down)(functools.partial(send_idx, down))
    for c in range(CHUNKS):
        ref = x_part(me, c)
        for at, going, to, recv in (
            (UP, has_up, up, xz_recv), (DOWN, has_down, down, xz_recv), (ACROSS, None, other, xy_recv),
        ):
            def go(ref=ref, at=at, to=to, recv=recv, c=c):
                remote(ref, ref, x_send.at[at], recv.at[line, c], to, core).start()
            if going is None:
                go()
            else:
                pl.when(going)(go)
    par_copies = [
        remote(w_src_all.at[core], w_src_all.at[core], par_send.at[0], par_recv.at[0], me, mate),
        remote(bias_all.at[core], bias_all.at[core], par_send.at[1], par_recv.at[1], me, mate),
        remote(embed_ref.at[mate_rows], embed_all.at[core], par_send.at[2], par_recv.at[2], me, mate),
        remote(w_node_all.at[core], w_node_all.at[core], par_send.at[3], par_recv.at[3], me, mate),
        remote(w_dec_all.at[core], w_dec_all.at[core], par_send.at[4], par_recv.at[4], me, mate),
    ]
    for copy in par_copies:
        copy.start()

    def tell(at, to):
        pl.semaphore_signal(ready.at[at], inc=1, device_id={"graph": to, "chan": core}, device_id_type=MESH)

    pl.when(line == 0)(functools.partial(tell, 0, up))
    pl.when(line == lines - 1)(functools.partial(tell, 1, down))

    def relays(part, send, z_recv, y_recv, late, arrived):
        def extra(q, to):
            shard = line * 2 + 1 - side
            ref = part(shard, q)
            remote(ref, ref, send.at[UP if to == "up" else DOWN], y_recv.at[line, q],
                   up if to == "up" else down, core).start()

        def extra_going(to, q):
            going, at, target_low = (
                (has_up, line + 1, line + 1 < lines // 2) if to == "up" else (has_down, line - 1, line - 1 < lines // 2)
            )
            full = target_low if to == "up" else jnp.logical_not(target_low)
            return going if late(q) else going & full

        def last_stage(to):
            return line - 1 if to == "up" else lines - 2 - line

        def extras(i, q):
            for to in ("up", "down"):
                pl.when(extra_going(to, q) & (last_stage(to) == i))(functools.partial(extra, q, to))

        def take_line(i, q, which):
            for above in (True, False):
                source = line + 1 + i if above else line - 1 - i
                valid = (source < lines) if above else (source >= 0)
                if which is not None:
                    valid = valid & ((low_half if above else jnp.logical_not(low_half)) == (which == "inner"))
                onward, to, at = (has_down, down, DOWN) if above else (has_up, up, UP)

                @pl.when(valid)
                def _(source=source, onward=onward, to=to, at=at):
                    ref = part(source * 2 + side, q)
                    remote(ref, ref, send.at[at], z_recv.at[source, q], me, mate).wait_recv()

                    @pl.when(onward)
                    def _():
                        remote(ref, ref, send.at[at], z_recv.at[source, q], to, core).start()

                    crossing = source != outer
                    if late(q):
                        crossing = crossing & (source != inner)

                    @pl.when(crossing)
                    def _():
                        remote(ref, ref, send.at[ACROSS], y_recv.at[source, q], other, core).start()

                    arrived(source * 2 + side, q)

        def take_other(i, q):
            def take(source):
                shard = source * 2 + 1 - side
                ref = part(shard, q)
                remote(ref, ref, send.at[ACROSS], y_recv.at[source, q], me, mate).wait_recv()
                arrived(shard, q)

            if i == 0:
                take(line)
                extras(-1, q)
                return
            for source, valid in ((line + i, line + i < lines), (line - i, line - i >= 0)):
                if late(q):
                    valid = valid & (source != inner)
                pl.when(valid)(functools.partial(take, source))

        def take_inner(q):
            shard = inner * 2 + 1 - side
            ref = part(shard, q)
            remote(ref, ref, send.at[ACROSS], y_recv.at[inner, q], me, mate).wait_recv()
            arrived(shard, q)

        return take_line, take_other, take_inner, extras

    def to_mate(shard, c):
        ref = x_part(shard, c)
        remote(ref, ref, x_send.at[MATE], xm_recv.at[shard], me, mate).start()

    nearest = [sorted((p for p in range(lines) if p != at), key=lambda p: (abs(p - at), p)) for at in range(lines)]
    build_order = [me, other]
    for i in range(lines - 1):
        source = by_line([nearest[at][i] for at in range(lines)])
        build_order += [source * 2 + side, source * 2 + 1 - side]
    tables = [arrival_order(at, lines) for at in range(lines)]
    order = []
    for k in range(peers - 1):
        source = by_line([tables[at][k][2] for at in range(lines)])
        flip = by_line([tables[at][k][3] for at in range(lines)])
        stage = max(tables[at][k][0] for at in range(lines))
        order.append((stage, source * 2 + jnp.where(flip == 1, 1 - side, side)))

    def build_enc(shard, wait=True):
        if wait:
            remote(idx_own.at[0], idx_in.at[shard], idx_send.at[0], idx_recv.at[shard], me, mate).wait_recv()
        hot[:half_mesh, :] = one_hot(core * half_mesh, half_mesh, dst_vmem[shard])
        for t in range(2):
            picks = one_hot(t * half_grid, half_grid, idx_in[shard, 0:1, :])
            enc[shard, :, t * half_grid : (t + 1) * half_grid] = lax.dot_general(
                hot[:half_mesh, :], picks, NT, preferred_element_type=jnp.float32
            ).astype(jnp.bfloat16)

    pending = []

    def dec_copy(shard, half):
        ref = dec.at[shard, pl.ds(pl.multiple_of(half * half_grid, half_grid), half_grid)]
        return remote(ref, ref, dec_send.at[0], dec_recv.at[shard], me, mate)

    def flush():
        while pending:
            dec_copy(pending.pop(0), core).start()

    def build_dec(shard):
        flush()
        hot[...] = one_hot(0, mesh_rows, idx_in[shard, 1:2, :])
        for t in range(half_grid // 256):
            first = pl.multiple_of(core * half_grid, half_grid) + t * 256
            picks = one_hot(first, 256, idx_own[shard, 0:1, :])
            dec[shard, pl.ds(pl.multiple_of(first, 256), 256), :] = lax.dot_general(
                picks, hot[...], NT, preferred_element_type=jnp.float32
            ).astype(jnp.bfloat16)
        pending.append(shard)

    def encode(shard, first=False):
        if not first:
            whole = x_all.at[pl.ds(0, half_grid)]
            remote(whole, whole, x_send.at[MATE], xm_recv.at[shard], me, mate).wait_recv()
        for c in range(CHUNKS):
            rows = pl.ds(pl.multiple_of(shard * grid_rows, grid_rows) + c * 2 * block, 2 * block)
            for h in range(2):
                pre = jnp.dot(x_all[rows, :], w_src_all[h], preferred_element_type=jnp.float32) + bias_all[h]
                msg[c * 2 * block : (c + 1) * 2 * block, h * (msg.shape[1] // 2) : (h + 1) * (msg.shape[1] // 2)] = (
                    pre + pre * jnp.tanh(pre)
                ).astype(jnp.bfloat16)
        total = jnp.dot(enc[shard], msg[...], preferred_element_type=jnp.float32)
        if first:
            agg[...] = total
        else:
            agg[...] += total

    build_enc(me, wait=False)
    for copy in par_copies:
        copy.wait()
    w_src_all[...] = w_src_all[...] * 0.5
    bias_all[...] = bias_all[...] * 0.5
    encode(me, first=True)

    @pl.when(has_down)
    def _():
        pl.semaphore_wait(ready.at[0], 1)
        pl.when(has_up)(functools.partial(tell, 0, up))

    @pl.when(has_up)
    def _():
        pl.semaphore_wait(ready.at[1], 1)
        pl.when(has_down)(functools.partial(tell, 1, down))

    for source in range(lines):
        for its_side in range(2):
            to = source * 2 + its_side
            same = side == its_side
            near = jnp.where(same, jnp.abs(line - source) <= 1, line == source)
            pl.when(jnp.logical_not(near))(functools.partial(send_idx, to))

    tasks = [functools.partial(build_enc, shard) for shard in build_order[1:]]
    dec_tasks = [functools.partial(build_dec, shard) for shard in build_order]

    def run(count):
        for _ in range(count):
            if tasks:
                tasks.pop(0)()
            elif dec_tasks:
                dec_tasks.pop(0)()

    def halves(c):
        return c >= CHUNKS // 2

    take_line, take_other, take_inner, extras = relays(x_part, x_send, xz_recv, xy_recv, halves, to_mate)
    for i in range(lines):
        for c in range(CHUNKS):
            if i < lines - 1:
                take_line(i, c, None)
            take_other(i, c)
            if i < lines - 1:
                run(-(-len(tasks) // (CHUNKS - c)) if i else 1)
            elif tasks:
                run(1)
        for c in range(CHUNKS):
            extras(i, c)
        tasks.extend(functools.partial(encode, shard) for stage, shard in order if stage == i)
    for c in range(CHUNKS // 2, CHUNKS):
        take_inner(c)
    tasks.extend(functools.partial(encode, shard) for stage, shard in order if stage == lines)
    while tasks:
        tasks.pop(0)()

    hidden_cols = agg.shape[1]
    width = hidden_cols // 2
    hidden = sum(
        jnp.dot(agg[:, h * width : (h + 1) * width].astype(jnp.bfloat16), w_node_all[h], preferred_element_type=jnp.float32)
        for h in range(2)
    )
    projected = sum(
        jnp.dot(
            (
                embed_all[h].astype(jnp.float32) + silu(hidden[:, h * width : (h + 1) * width])
            ).astype(jnp.bfloat16),
            w_dec_all[h], preferred_element_type=jnp.float32,
        )
        for h in range(2)
    ).astype(jnp.bfloat16)
    my_first = pl.multiple_of(me * mesh_rows + core * half_mesh, half_mesh)

    @pl.when(core == 0)
    def _():
        proj_all[pl.ds(my_first, half_mesh), :] = projected[:, :cols]
        proj_mate[...] = projected[:, cols:]

    @pl.when(core == 1)
    def _():
        proj_all[pl.ds(my_first, half_mesh), :] = projected[:, cols:]
        proj_mate[...] = projected[:, :cols]

    def p_part(shard, q):
        flip, sub = q % 2, q // 2
        half = mate if flip else core
        first = shard * mesh_rows + half * half_mesh + sub * part_mesh
        return proj_all.at[pl.ds(pl.multiple_of(first, part_mesh), part_mesh)]

    for sub in range(SUBS):
        into = p_part(me, 2 * sub)
        for flip in range(2):
            ref = proj_mate.at[pl.ds(sub * part_mesh, part_mesh)] if flip else into
            chan = mate if flip else core
            for at, going, to, recv in (
                (UP, has_up, up, pz_recv), (DOWN, has_down, down, pz_recv), (ACROSS, None, other, py_recv),
            ):
                def go(ref=ref, into=into, at=at, to=to, recv=recv, q=2 * sub + flip, chan=chan):
                    remote(ref, into, p_send.at[at], recv.at[line, q], to, chan).start()
                if going is None:
                    go()
                else:
                    pl.when(going)(go)
    whole_half = proj_all.at[pl.ds(my_first, half_mesh)]
    remote(proj_mate, whole_half, p_send.at[MATE], pm_recv.at[0], me, mate).start()

    def decode(shard, first=False):
        remote(dec.at[0, pl.ds(0, half_grid)], dec.at[0, pl.ds(0, half_grid)], dec_send.at[0], dec_recv.at[shard], me, mate).wait_recv()
        rows = pl.ds(pl.multiple_of(shard * mesh_rows, mesh_rows), mesh_rows)
        for t in range(2):
            at = pl.ds(t * half_grid, half_grid)
            acc[at, :] += jnp.dot(dec[shard, at, :], proj_all[rows, :], preferred_element_type=jnp.float32)

    tasks = dec_tasks[:]
    take_line, take_other, take_inner, extras = relays(
        p_part, p_send, pz_recv, py_recv, lambda q: q >= SUBS, lambda shard, q: None)
    acc[...] = x_all[own_rows, pl.ds(pl.multiple_of(core * cols, cols), cols)].astype(jnp.float32)

    def own_decode():
        remote(proj_mate, whole_half, p_send.at[MATE], pm_recv.at[0], me, mate).wait_recv()
        decode(me)

    tasks.append(flush)
    tasks.append(own_decode)
    late_tasks = []
    for _ in range(2):
        tasks.pop(0)()
    pieces = 2 * SUBS
    for i in range(lines):
        if i < lines - 1:
            for q in range(pieces):
                take_line(i, q, "inner")
                if tasks and q % 2:
                    tasks.pop(0)()
        for q in range(pieces):
            take_other(i, q)
            if i < lines - 1:
                take_line(i, q, "outer")
            if tasks:
                tasks.pop(0)()
        for q in range(pieces):
            extras(i, q)
        tasks.extend(functools.partial(decode, shard) for stage, shard in order if stage == i)
    for q in range(SUBS, pieces):
        take_inner(q)
    tasks.extend(functools.partial(decode, shard) for stage, shard in order if stage == lines)
    while tasks:
        tasks.pop(0)()
    out_ref[...] = acc[...].astype(jnp.bfloat16)

    def drained(ref, sem):
        remote(ref, ref, sem, sem, me, mate).wait_send()

    for at in range(lines):
        @pl.when(line == at)
        def _(at=at):
            for n, (x_n, p_n) in enumerate(zip(link_pieces(at, lines, CHUNKS), link_pieces(at, lines, pieces))):
                if x_n:
                    drained(x_all.at[pl.ds(0, x_n * block)], x_send.at[n])
                    drained(proj_all.at[pl.ds(0, p_n * part_mesh)], p_send.at[n])
    drained(x_all.at[pl.ds(0, (peers - 1) * half_grid)], x_send.at[MATE])
    drained(proj_mate, p_send.at[MATE])
    drained(idx_own.at[pl.ds(0, peers - 1)], idx_send.at[0])
    drained(dec.at[:, pl.ds(0, half_grid)], dec_send.at[0])


def fused(grid_state, w_src, bias_src, mesh_embed, w_node, w_dec, slot_src, slot_dst, slot_count):
    peers = lax.axis_size("graph")
    capacity = slot_src.shape[2]
    grid_rows, chans = grid_state.shape
    mesh_rows = mesh_embed.shape[0]
    hidden = w_src.shape[1]
    lines = peers // 2
    bf16, f32, i32 = jnp.bfloat16, jnp.float32, jnp.int32
    dma = pltpu.SemaphoreType.DMA
    pieces = 2 * SUBS
    return pl.pallas_call(
        functools.partial(graph_kernel, peers),
        out_shape=jax.ShapeDtypeStruct((grid_rows, chans // 2), bf16),
        in_specs=[pl.BlockSpec(memory_space=pl.ANY)] * 9,
        out_specs=pl.BlockSpec(memory_space=pltpu.VMEM),
        scratch_shapes=[
            pltpu.VMEM((peers * grid_rows, chans), bf16),
            pltpu.VMEM((peers, 2, capacity), i32),
            pltpu.VMEM((peers, 2, capacity), i32),
            pltpu.VMEM(slot_src.shape, i32),
            pltpu.VMEM(slot_dst.shape, i32),
            pltpu.SMEM(slot_count.shape, i32),
            pltpu.VMEM((2,) + w_src.shape, bf16),
            pltpu.VMEM((2, 1, hidden), f32),
            pltpu.VMEM((2, mesh_rows // 2, hidden), bf16),
            pltpu.VMEM((2,) + w_node.shape, bf16),
            pltpu.VMEM((2,) + w_dec.shape, bf16),
            pltpu.VMEM((peers, mesh_rows // 2, grid_rows), bf16),
            pltpu.VMEM((peers, grid_rows, mesh_rows), bf16),
            pltpu.VMEM((mesh_rows, capacity), HOT),
            pltpu.VMEM((grid_rows, 2 * hidden), bf16),
            pltpu.VMEM((mesh_rows // 2, 2 * hidden), f32),
            pltpu.VMEM((grid_rows, chans // 2), f32),
            pltpu.VMEM((mesh_rows // 2, chans // 2), bf16),
            pltpu.VMEM((peers * mesh_rows, chans // 2), bf16),
            pltpu.SemaphoreType.REGULAR((2,)),
            dma((9,)), dma((5,)), dma((5,)), dma((1,)), dma((peers,)),
            dma((4,)), dma((lines, CHUNKS)), dma((lines, CHUNKS)), dma((peers,)),
            dma((4,)), dma((lines, pieces)), dma((lines, pieces)), dma((1,)), dma((1,)), dma((peers,)),
        ],
        compiler_params=pltpu.CompilerParams(collective_id=0, has_side_effects=True),
    )(grid_state, w_src, bias_src[None, :], mesh_embed, w_node, w_dec, slot_src, slot_dst, slot_count)


def held_bytes(peers, grid_state, mesh_embed, *rest):
    grid_rows, chans = grid_state.shape
    mesh_rows = mesh_embed.shape[0]
    return 2 * peers * grid_rows * (chans + 2 * mesh_rows)


def per_device(grid_state, w_src, bias_src, mesh_embed, *rest):
    peers = lax.axis_size("graph")
    fits = (
        peers % 2 == 0
        and peers >= 4
        and lax.axis_size("chan") == 2
        and held_bytes(peers, grid_state, mesh_embed) <= VMEM_BUDGET
    )
    body = fused if fits else on_device
    return body(grid_state, w_src, bias_src, mesh_embed, *rest)


def solution(mesh):
    placed = (
        P(("member", "graph"), None),
        P(None, "chan"),
        P("chan"),
        P("graph", "chan"),
        P("chan", None),
        P("chan", None),
        P("graph", None, None),
        P(None, "graph", None),
        P(),
    )
    return jax.shard_map(
        per_device,
        mesh=mesh,
        in_specs=placed,
        out_specs=P(("member", "graph"), "chan"),
        check_vma=False,
    )
```

time: 66.7 us -> 51.4 us (0.77)
  Pallas kernels: 64.7 us -> 49.6 us
  other arithmetic: 1.77 us -> 0 us
  local copies, waits for them, and re-layouts: 0 us -> 1.67 us
    pallas_call x1, Pallas kernels: 64.7 us -> 49.6 us  [fused(): pl.pallas_call(functools.partial(graph_kernel, peers), out_shape=jax.Shap...]
    convert_element_type x1 -> x0, other arithmetic: 1.77 us -> none  [fused(): return pl.pallas_call(functools.partial(graph_kernel, peers), out_shape=j...]
    unnamed x0 -> x1, local copies, waits for them, and re-layouts: none -> 1.67 us
where the time goes in v1:
time: 51.4 us; the launch traced here: 51.2 us
  Pallas kernels  49.6 us (96%)
  local copies, waits for them, and re-layouts  1.67 us (3%)
    pallas_call x1, Pallas kernels, fused(): pl.pallas_call(functools.partial(graph_kernel, peers), out_shape=jax.Shap...  49.6 us
    unnamed x1, local copies, waits for them, and re-layouts  1.67 us

profile of v1, /device:TPU:0, one launch (start us, length us, event | category | flops | bytes accessed | tf_op | source)
XLA Modules:
  0.0 51.2 jit_solution(10649204519902873482)
XLA Ops:
  0.0 49.6 %shard_map.91 = bf16[1024,128]{1,0:T(8,128)(2,1)} custom-call(bf16[1024,256]{1,0:T(8,128)(2,1)} %x_ref.1, bf16[256,256]{1,0:T(8,128)(2,1)} %w_src_ref.1, f32[1,256]{1,0:T(1,128)} %bitcast.1, bf16[640,256]{1,0:T(8,128)(2,1)} %embed_ref.1, bf16[256,512]{1,0:T(8,128)(2,1)} %w_node_ref.1, bf16[256,256]{1,0:T(8,128)(2,1)} %w_dec_ref.1, s32[1,8,1024]{2,1,0:T(8,128)} %src_ref.1, ...), custom_call_target="tpu_custom_call" | custom-call | tf_op jit(solution)/shard_map/pallas_call | solution.py:556
  49.6 1.7 %copy.11 = bf16[1024,128]{1,0:T(8,128)(2,1)} copy(bf16[1024,128]{1,0:T(8,128)(2,1)} %shard_map.91) | data formatting | bytes 524288

commit v2 on v1

--- a/solution.py
+++ b/solution.py
@@ -95,35 +95,42 @@
     return jnp.where(row_ids == indices, 1.0, 0.0).astype(HOT)
 
 
-def inner_of(line, lines):
-    return line + 1 if line < lines // 2 else line - 1
-
-
-def outer_of(line, lines):
-    return line - 1 if line < lines // 2 else line + 1
+def far_of(line, lines):
+    return lines - 1 if line < lines // 2 else 0
+
+
+def is_end(line, lines):
+    return line in (0, lines - 1)
+
+
+def given(line, lines):
+    outer = line - 1 if line < lines // 2 else line + 1
+    return outer if not is_end(line, lines) and is_end(outer, lines) else None
 
 
 def arrival_order(line, lines):
-    stages = [(0, 0, line, 1)]
+    stages = [(0, 1, 0, line)]
     for source in range(lines):
         gap = abs(source - line)
         if gap:
-            stages.append((gap - 1, gap, source, 0))
-            stages.append((lines if source == inner_of(line, lines) else gap, gap, source, 1))
-    return sorted(stages, key=lambda at: (at[0], at[3], at[1], at[2]))
+            split = is_end(line, lines) and source == far_of(line, lines)
+            stages += [(gap - 1, 0, gap, source), (lines if split else gap, 1, gap, source)]
+    return sorted(stages)
 
 
 def link_pieces(line, lines, pieces):
-    inner, outer = inner_of(line, lines), outer_of(line, lines)
-
     def extra(to):
-        return pieces if outer_of(to, lines) == line else pieces // 2 if inner_of(to, lines) == line else 0
+        if not 0 <= to < lines:
+            return 0
+        return pieces // 2 if is_end(to, lines) else pieces if given(to, lines) == line else 0
 
     up = pieces * (line + 1) + extra(line + 1) if line < lines - 1 else 0
     down = pieces * (lines - line) + extra(line - 1) if line > 0 else 0
-    across = pieces * lines - sum(
-        pieces if p == outer else pieces - pieces // 2 if p == inner else 0 for p in range(lines) if p != line
-    )
+    across = pieces * lines
+    if given(line, lines) is not None:
+        across -= pieces
+    if is_end(line, lines):
+        across -= pieces // 2
     return up, down, across
 
 
@@ -164,8 +171,9 @@
     def by_line(values):
         return sum(jnp.where(line == at, values[at], 0) for at in range(lines))
 
-    inner = jnp.where(low_half, line + 1, line - 1)
-    outer = jnp.where(low_half, line - 1, line + 1)
+    end = (line == 0) | (line == lines - 1)
+    far = jnp.where(low_half, lines - 1, 0)
+    giver = by_line([-1 if given(at, lines) is None else given(at, lines) for at in range(lines)])
     barrier = pltpu.get_barrier_semaphore()
 
     def greet(graph, chan):
@@ -213,17 +221,21 @@
     send_idx(other)
     pl.when(has_up)(functools.partial(send_idx, up))
     pl.when(has_down)(functools.partial(send_idx, down))
-    for c in range(CHUNKS):
+
+    def send_own(c):
         ref = x_part(me, c)
         for at, going, to, recv in (
             (UP, has_up, up, xz_recv), (DOWN, has_down, down, xz_recv), (ACROSS, None, other, xy_recv),
         ):
-            def go(ref=ref, at=at, to=to, recv=recv, c=c):
+            def go(at=at, to=to, recv=recv):
                 remote(ref, ref, x_send.at[at], recv.at[line, c], to, core).start()
             if going is None:
                 go()
             else:
                 pl.when(going)(go)
+
+    for c in range(CHUNKS // 2):
+        send_own(c)
     par_copies = [
         remote(w_src_all.at[core], w_src_all.at[core], par_send.at[0], par_recv.at[0], me, mate),
         remote(bias_all.at[core], bias_all.at[core], par_send.at[1], par_recv.at[1], me, mate),
@@ -241,25 +253,24 @@
     pl.when(line == lines - 1)(functools.partial(tell, 1, down))
 
     def relays(part, send, z_recv, y_recv, late, arrived):
-        def extra(q, to):
-            shard = line * 2 + 1 - side
-            ref = part(shard, q)
-            remote(ref, ref, send.at[UP if to == "up" else DOWN], y_recv.at[line, q],
-                   up if to == "up" else down, core).start()
-
-        def extra_going(to, q):
-            going, at, target_low = (
-                (has_up, line + 1, line + 1 < lines // 2) if to == "up" else (has_down, line - 1, line - 1 < lines // 2)
-            )
-            full = target_low if to == "up" else jnp.logical_not(target_low)
-            return going if late(q) else going & full
-
-        def last_stage(to):
-            return line - 1 if to == "up" else lines - 2 - line
-
-        def extras(i, q):
-            for to in ("up", "down"):
-                pl.when(extra_going(to, q) & (last_stage(to) == i))(functools.partial(extra, q, to))
+        def extra(source, q, above):
+            ref = part(source * 2 + 1 - side, q)
+            remote(ref, ref, send.at[UP if above else DOWN], y_recv.at[source, q], up if above else down, core).start()
+
+        def extras(source, q):
+            for above, there in ((True, has_up), (False, has_down)):
+                to = line + 1 if above else line - 1
+                to_end = (to == 0) | (to == lines - 1)
+                to_giver = by_line([
+                    -1 if not 0 <= at + (1 if above else -1) < lines
+                    or given(at + (1 if above else -1), lines) is None
+                    else given(at + (1 if above else -1), lines)
+                    for at in range(lines)
+                ])
+                wanted = (source == line) & (to_giver == line)
+                if late(q):
+                    wanted = wanted | (to_end & (source == jnp.where(to < lines // 2, lines - 1, 0)))
+                pl.when(there & wanted)(functools.partial(extra, source, q, above))
 
         def take_line(i, q, which):
             for above in (True, False):
@@ -278,9 +289,9 @@
                     def _():
                         remote(ref, ref, send.at[at], z_recv.at[source, q], to, core).start()
 
-                    crossing = source != outer
+                    crossing = source != giver
                     if late(q):
-                        crossing = crossing & (source != inner)
+                        crossing = crossing & jnp.logical_not(end & (source == far))
 
                     @pl.when(crossing)
                     def _():
@@ -293,28 +304,31 @@
                 shard = source * 2 + 1 - side
                 ref = part(shard, q)
                 remote(ref, ref, send.at[ACROSS], y_recv.at[source, q], me, mate).wait_recv()
+                extras(source, q)
                 arrived(shard, q)
 
             if i == 0:
                 take(line)
-                extras(-1, q)
                 return
             for source, valid in ((line + i, line + i < lines), (line - i, line - i >= 0)):
                 if late(q):
-                    valid = valid & (source != inner)
+                    valid = valid & jnp.logical_not(end & (source == far))
                 pl.when(valid)(functools.partial(take, source))
 
-        def take_inner(q):
-            shard = inner * 2 + 1 - side
+        def take_far(q):
+            pl.when(end)(functools.partial(take_one, far, q))
+
+        def take_one(source, q):
+            shard = source * 2 + 1 - side
             ref = part(shard, q)
-            remote(ref, ref, send.at[ACROSS], y_recv.at[inner, q], me, mate).wait_recv()
+            remote(ref, ref, send.at[ACROSS], y_recv.at[source, q], me, mate).wait_recv()
             arrived(shard, q)
 
-        return take_line, take_other, take_inner, extras
+        return take_line, take_other, take_far
 
     def to_mate(shard, c):
         ref = x_part(shard, c)
-        remote(ref, ref, x_send.at[MATE], xm_recv.at[shard], me, mate).start()
+        remote(ref, ref, x_send.at[MATE], xm_recv.at[shard, c // (CHUNKS // 2)], me, mate).start()
 
     nearest = [sorted((p for p in range(lines) if p != at), key=lambda p: (abs(p - at), p)) for at in range(lines)]
     build_order = [me, other]
@@ -324,8 +338,8 @@
     tables = [arrival_order(at, lines) for at in range(lines)]
     order = []
     for k in range(peers - 1):
-        source = by_line([tables[at][k][2] for at in range(lines)])
-        flip = by_line([tables[at][k][3] for at in range(lines)])
+        source = by_line([tables[at][k][3] for at in range(lines)])
+        flip = by_line([tables[at][k][1] for at in range(lines)])
         stage = max(tables[at][k][0] for at in range(lines))
         order.append((stage, source * 2 + jnp.where(flip == 1, 1 - side, side)))
 
@@ -349,7 +363,7 @@
         while pending:
             dec_copy(pending.pop(0), core).start()
 
-    def build_dec(shard):
+    def build_dec(shard, wait=True):
         flush()
         hot[...] = one_hot(0, mesh_rows, idx_in[shard, 1:2, :])
         for t in range(half_grid // 256):
@@ -360,105 +374,95 @@
             ).astype(jnp.bfloat16)
         pending.append(shard)
 
-    def encode(shard, first=False):
+    def encode(shard, first=False, parts=(0, 1)):
         if not first:
-            whole = x_all.at[pl.ds(0, half_grid)]
-            remote(whole, whole, x_send.at[MATE], xm_recv.at[shard], me, mate).wait_recv()
-        for c in range(CHUNKS):
+            for part in parts:
+                some = x_all.at[pl.ds(0, half_grid // 2)]
+                remote(some, some, x_send.at[MATE], xm_recv.at[shard, part], me, mate).wait_recv()
+        low, high = min(parts) * CHUNKS // 2, (max(parts) + 1) * CHUNKS // 2
+        for c in range(low, high):
             rows = pl.ds(pl.multiple_of(shard * grid_rows, grid_rows) + c * 2 * block, 2 * block)
             for h in range(2):
                 pre = jnp.dot(x_all[rows, :], w_src_all[h], preferred_element_type=jnp.float32) + bias_all[h]
                 msg[c * 2 * block : (c + 1) * 2 * block, h * (msg.shape[1] // 2) : (h + 1) * (msg.shape[1] // 2)] = (
                     pre + pre * jnp.tanh(pre)
                 ).astype(jnp.bfloat16)
-        total = jnp.dot(enc[shard], msg[...], preferred_element_type=jnp.float32)
+        some = slice(low * 2 * block, high * 2 * block)
+        total = jnp.dot(enc[shard, :, some], msg[some, :], preferred_element_type=jnp.float32)
         if first:
             agg[...] = total
         else:
             agg[...] += total
 
+    def poll(hop):
+        @pl.when(line == hop + 1)
+        def _():
+            pl.semaphore_wait(ready.at[0], 1)
+            pl.when(has_up)(functools.partial(tell, 0, up))
+
+        @pl.when(line == lines - 2 - hop)
+        def _():
+            pl.semaphore_wait(ready.at[1], 1)
+            pl.when(has_down)(functools.partial(tell, 1, down))
+
+        known = by_line([max(at - 1, lines - 2 - at) for at in range(lines)]) == hop
+        for source in range(lines):
+            for its_side in range(2):
+                near = jnp.where(side == its_side, jnp.abs(line - source), 2 * jnp.abs(line - source) + 1) <= 1
+                pl.when(known & jnp.logical_not(near))(functools.partial(send_idx, source * 2 + its_side))
+
+    poll(0)
     build_enc(me, wait=False)
+    build_dec(me, wait=False)
+    poll(1)
+    for c in range(CHUNKS // 2, CHUNKS - 1):
+        send_own(c)
     for copy in par_copies:
         copy.wait()
     w_src_all[...] = w_src_all[...] * 0.5
     bias_all[...] = bias_all[...] * 0.5
     encode(me, first=True)
-
-    @pl.when(has_down)
-    def _():
-        pl.semaphore_wait(ready.at[0], 1)
-        pl.when(has_up)(functools.partial(tell, 0, up))
-
-    @pl.when(has_up)
-    def _():
-        pl.semaphore_wait(ready.at[1], 1)
-        pl.when(has_down)(functools.partial(tell, 1, down))
-
-    for source in range(lines):
-        for its_side in range(2):
-            to = source * 2 + its_side
-            same = side == its_side
-            near = jnp.where(same, jnp.abs(line - source) <= 1, line == source)
-            pl.when(jnp.logical_not(near))(functools.partial(send_idx, to))
-
-    tasks = [functools.partial(build_enc, shard) for shard in build_order[1:]]
-    dec_tasks = [functools.partial(build_dec, shard) for shard in build_order]
+    for hop in range(2, lines - 1):
+        poll(hop)
+    for c in range(CHUNKS - 1, CHUNKS):
+        send_own(c)
+    enc_tasks = [functools.partial(build_enc, shard) for shard in build_order[1:]]
+    dec_tasks = [functools.partial(build_dec, shard, wait=False) for shard in build_order[1:]]
+    tasks = [task for pair in zip(enc_tasks[:-2], dec_tasks[:-2]) for task in pair] + enc_tasks[-2:]
+    dec_tasks = dec_tasks[-2:]
 
     def run(count):
-        for _ in range(count):
-            if tasks:
-                tasks.pop(0)()
-            elif dec_tasks:
-                dec_tasks.pop(0)()
+        for _ in range(min(count, len(tasks))):
+            tasks.pop(0)()
 
     def halves(c):
         return c >= CHUNKS // 2
 
-    take_line, take_other, take_inner, extras = relays(x_part, x_send, xz_recv, xy_recv, halves, to_mate)
+    take_line, take_other, take_far = relays(x_part, x_send, xz_recv, xy_recv, halves, to_mate)
+    def encodes(stage, parts):
+        return [functools.partial(encode, shard, parts=parts) for at, shard in order if at == stage]
+
+    run(2)
     for i in range(lines):
         for c in range(CHUNKS):
             if i < lines - 1:
                 take_line(i, c, None)
             take_other(i, c)
-            if i < lines - 1:
-                run(-(-len(tasks) // (CHUNKS - c)) if i else 1)
-            elif tasks:
-                run(1)
-        for c in range(CHUNKS):
-            extras(i, c)
-        tasks.extend(functools.partial(encode, shard) for stage, shard in order if stage == i)
+            if i == lines - 2 and c == CHUNKS // 2:
+                tasks.append(dec_tasks.pop(0))
+                tasks += encodes(i, (0,))
+            if i == lines - 1 and c == CHUNKS // 2:
+                tasks += encodes(lines, (0,))
+            run(1 + c // 2 if i == 0 else -(-len(tasks) // (CHUNKS - c)))
+        tasks += encodes(i, (1,) if i == lines - 2 else (0, 1))
     for c in range(CHUNKS // 2, CHUNKS):
-        take_inner(c)
-    tasks.extend(functools.partial(encode, shard) for stage, shard in order if stage == lines)
-    while tasks:
-        tasks.pop(0)()
-
-    hidden_cols = agg.shape[1]
-    width = hidden_cols // 2
-    hidden = sum(
-        jnp.dot(agg[:, h * width : (h + 1) * width].astype(jnp.bfloat16), w_node_all[h], preferred_element_type=jnp.float32)
-        for h in range(2)
-    )
-    projected = sum(
-        jnp.dot(
-            (
-                embed_all[h].astype(jnp.float32) + silu(hidden[:, h * width : (h + 1) * width])
-            ).astype(jnp.bfloat16),
-            w_dec_all[h], preferred_element_type=jnp.float32,
-        )
-        for h in range(2)
-    ).astype(jnp.bfloat16)
+        take_far(c)
+    run(len(tasks))
+    for task in encodes(lines, (1,)):
+        task()
+
+    width = agg.shape[1] // 2
     my_first = pl.multiple_of(me * mesh_rows + core * half_mesh, half_mesh)
-
-    @pl.when(core == 0)
-    def _():
-        proj_all[pl.ds(my_first, half_mesh), :] = projected[:, :cols]
-        proj_mate[...] = projected[:, cols:]
-
-    @pl.when(core == 1)
-    def _():
-        proj_all[pl.ds(my_first, half_mesh), :] = projected[:, cols:]
-        proj_mate[...] = projected[:, :cols]
 
     def p_part(shard, q):
         flip, sub = q % 2, q // 2
@@ -467,7 +471,29 @@
         return proj_all.at[pl.ds(pl.multiple_of(first, part_mesh), part_mesh)]
 
     for sub in range(SUBS):
+        some = slice(sub * part_mesh, (sub + 1) * part_mesh)
+        hidden = sum(
+            jnp.dot(
+                agg[some, h * width : (h + 1) * width].astype(jnp.bfloat16), w_node_all[h],
+                preferred_element_type=jnp.float32,
+            )
+            for h in range(2)
+        )
+        projected = sum(
+            jnp.dot(
+                (
+                    embed_all[h, some, :].astype(jnp.float32) + silu(hidden[:, h * width : (h + 1) * width])
+                ).astype(jnp.bfloat16),
+                w_dec_all[h], preferred_element_type=jnp.float32,
+            )
+            for h in range(2)
+        ).astype(jnp.bfloat16)
+        first_core = core == 0
         into = p_part(me, 2 * sub)
+        proj_all[pl.ds(pl.multiple_of(my_first + sub * part_mesh, part_mesh), part_mesh), :] = jnp.where(
+            first_core, projected[:, :cols], projected[:, cols:]
+        )
+        proj_mate[some, :] = jnp.where(first_core, projected[:, cols:], projected[:, :cols])
         for flip in range(2):
             ref = proj_mate.at[pl.ds(sub * part_mesh, part_mesh)] if flip else into
             chan = mate if flip else core
@@ -491,7 +517,7 @@
             acc[at, :] += jnp.dot(dec[shard, at, :], proj_all[rows, :], preferred_element_type=jnp.float32)
 
     tasks = dec_tasks[:]
-    take_line, take_other, take_inner, extras = relays(
+    take_line, take_other, take_far = relays(
         p_part, p_send, pz_recv, py_recv, lambda q: q >= SUBS, lambda shard, q: None)
     acc[...] = x_all[own_rows, pl.ds(pl.multiple_of(core * cols, cols), cols)].astype(jnp.float32)
 
@@ -500,28 +526,26 @@
         decode(me)
 
     tasks.append(flush)
+    pieces = 2 * SUBS
+    while tasks:
+        tasks.pop(0)()
     tasks.append(own_decode)
-    late_tasks = []
-    for _ in range(2):
-        tasks.pop(0)()
-    pieces = 2 * SUBS
     for i in range(lines):
         if i < lines - 1:
-            for q in range(pieces):
-                take_line(i, q, "inner")
-                if tasks and q % 2:
-                    tasks.pop(0)()
+            for q in range(pieces + 1):
+                if q < pieces:
+                    take_line(i, q, "inner")
+                if q:
+                    take_line(i, q - 1, "outer")
         for q in range(pieces):
             take_other(i, q)
-            if i < lines - 1:
-                take_line(i, q, "outer")
-            if tasks:
+            if tasks and i:
                 tasks.pop(0)()
-        for q in range(pieces):
-            extras(i, q)
+        while tasks and i == 0:
+            tasks.pop(0)()
         tasks.extend(functools.partial(decode, shard) for stage, shard in order if stage == i)
     for q in range(SUBS, pieces):
-        take_inner(q)
+        take_far(q)
     tasks.extend(functools.partial(decode, shard) for stage, shard in order if stage == lines)
     while tasks:
         tasks.pop(0)()
@@ -580,7 +604,7 @@
             pltpu.VMEM((peers * mesh_rows, chans // 2), bf16),
             pltpu.SemaphoreType.REGULAR((2,)),
             dma((9,)), dma((5,)), dma((5,)), dma((1,)), dma((peers,)),
-            dma((4,)), dma((lines, CHUNKS)), dma((lines, CHUNKS)), dma((peers,)),
+            dma((4,)), dma((lines, CHUNKS)), dma((lines, CHUNKS)), dma((peers, 2)),
             dma((4,)), dma((lines, pieces)), dma((lines, pieces)), dma((1,)), dma((1,)), dma((peers,)),
         ],
         compiler_params=pltpu.CompilerParams(collective_id=0, has_side_effects=True),

time: 51.4 us -> 49.9 us (0.971)
  Pallas kernels: 49.6 us -> 48.1 us
    pallas_call x1, Pallas kernels: 49.6 us -> 48.1 us  [fused(): pl.pallas_call(functools.partial(graph_kernel, peers), out_shape=jax.Shap...]
where the time goes in v2:
time: 49.9 us; the launch traced here: 49.8 us
  Pallas kernels  48.1 us (96%)
  local copies, waits for them, and re-layouts  1.67 us (3%)
    pallas_call x1, Pallas kernels, fused(): pl.pallas_call(functools.partial(graph_kernel, peers), out_shape=jax.Shap...  48.1 us
    unnamed x1, local copies, waits for them, and re-layouts  1.67 us

profile of v2, /device:TPU:0, one launch (start us, length us, event | category | flops | bytes accessed | tf_op | source)
XLA Modules:
  0.0 49.8 jit_solution(6518469366611085043)
XLA Ops:
  0.0 48.1 %shard_map.91 = bf16[1024,128]{1,0:T(8,128)(2,1)} custom-call(bf16[1024,256]{1,0:T(8,128)(2,1)} %x_ref.1, bf16[256,256]{1,0:T(8,128)(2,1)} %w_src_ref.1, f32[1,256]{1,0:T(1,128)} %bitcast.1, bf16[640,256]{1,0:T(8,128)(2,1)} %embed_ref.1, bf16[256,512]{1,0:T(8,128)(2,1)} %w_node_ref.1, bf16[256,256]{1,0:T(8,128)(2,1)} %w_dec_ref.1, s32[1,8,1024]{2,1,0:T(8,128)} %src_ref.1, ...), custom_call_target="tpu_custom_call" | custom-call | tf_op jit(solution)/shard_map/pallas_call | solution.py:580
  48.1 1.7 %copy.11 = bf16[1024,128]{1,0:T(8,128)(2,1)} copy(bf16[1024,128]{1,0:T(8,128)(2,1)} %shard_map.91) | data formatting | bytes 524288

commit v3 on v2

--- a/solution.py
+++ b/solution.py
@@ -91,12 +91,9 @@
 
 
 def one_hot(first, rows, indices):
-    row_ids = lax.broadcasted_iota(jnp.int32, (rows, indices.shape[1]), 0) + first
-    return jnp.where(row_ids == indices, 1.0, 0.0).astype(HOT)
-
-
-def far_of(line, lines):
-    return lines - 1 if line < lines // 2 else 0
+    row_ids = lax.broadcasted_iota(jnp.int16, (rows, indices.shape[1]), 0)
+    hits = row_ids == (indices - first).astype(jnp.int16)
+    return jnp.where(hits, jnp.bfloat16(1), jnp.bfloat16(0)).astype(HOT)
 
 
 def is_end(line, lines):
@@ -113,7 +110,7 @@
     for source in range(lines):
         gap = abs(source - line)
         if gap:
-            split = is_end(line, lines) and source == far_of(line, lines)
+            split = is_end(line, lines) and gap > 1
             stages += [(gap - 1, 0, gap, source), (lines if split else gap, 1, gap, source)]
     return sorted(stages)
 
@@ -122,7 +119,7 @@
     def extra(to):
         if not 0 <= to < lines:
             return 0
-        return pieces // 2 if is_end(to, lines) else pieces if given(to, lines) == line else 0
+        return lines - 2 if is_end(to, lines) else pieces if given(to, lines) == line else 0
 
     up = pieces * (line + 1) + extra(line + 1) if line < lines - 1 else 0
     down = pieces * (lines - line) + extra(line - 1) if line > 0 else 0
@@ -130,8 +127,33 @@
     if given(line, lines) is not None:
         across -= pieces
     if is_end(line, lines):
-        across -= pieces // 2
+        across -= lines - 2
     return up, down, across
+
+
+def return_order(line, lines):
+    stages = [(0, 1, 0, line)]
+    for source in range(lines):
+        gap = abs(source - line)
+        if gap:
+            stages += [(gap - 1, 0, gap, source), (lines - 2 + gap, 1, gap, source)]
+    return sorted(stages)
+
+
+def return_pieces(line, lines, pieces):
+    direct = lines > 2
+
+    def one_way(to, behind, first):
+        if not 0 <= to < lines:
+            return 0
+        onward = behind - (1 if direct and is_end(to, lines) and behind else 0)
+        beside = pieces // 2 if is_end(to, lines) else pieces if given(to, lines) == line else 0
+        return pieces * (1 + (1 if direct and first else 0) + onward) + beside
+
+    up = one_way(line + 1, line, line == 0)
+    down = one_way(line - 1, lines - 1 - line, line == lines - 1)
+    skipped = pieces if given(line, lines) is not None else pieces // 2 if is_end(line, lines) else 0
+    return up, down, pieces * lines - skipped
 
 
 def graph_kernel(
@@ -172,7 +194,6 @@
         return sum(jnp.where(line == at, values[at], 0) for at in range(lines))
 
     end = (line == 0) | (line == lines - 1)
-    far = jnp.where(low_half, lines - 1, 0)
     giver = by_line([-1 if given(at, lines) is None else given(at, lines) for at in range(lines)])
     barrier = pltpu.get_barrier_semaphore()
 
@@ -198,29 +219,14 @@
         pltpu.make_async_copy(w_dec_ref, w_dec_all.at[core], local_sem.at[7]),
         pltpu.make_async_copy(embed_ref.at[my_rows], embed_all.at[core], local_sem.at[8]),
     ]
-    for copy in locals_:
+    for copy in locals_[3:4] + locals_[:3] + locals_[4:]:
         copy.start()
-    for copy in locals_[:3]:
-        copy.wait()
-    slots = lax.broadcasted_iota(jnp.int32, (1, capacity), 1)
-    for to in range(peers):
-        idx_own[to, 0:1, :] = jnp.where(slots < count_smem[me, to], src_vmem[0, to : to + 1, :], -1)
-        idx_own[to, 1:2, :] = dst_vmem[to]
-    idx_in[me] = idx_own[me]
-    for copy in locals_[3:]:
-        copy.wait()
+    locals_[3].wait()
     pl.semaphore_wait(barrier, 3 + 2 * jnp.where(has_up, 1, 0) + 2 * jnp.where(has_down, 1, 0))
-
-    def send_idx(to):
-        remote(idx_own.at[to], idx_in.at[me], idx_send.at[0], idx_recv.at[me], to, core).start()
 
     def x_part(shard, c, half=core):
         first = shard * grid_rows + c * 2 * block + half * block
         return x_all.at[pl.ds(pl.multiple_of(first, block), block)]
-
-    send_idx(other)
-    pl.when(has_up)(functools.partial(send_idx, up))
-    pl.when(has_down)(functools.partial(send_idx, down))
 
     def send_own(c):
         ref = x_part(me, c)
@@ -234,8 +240,25 @@
             else:
                 pl.when(going)(go)
 
-    for c in range(CHUNKS // 2):
+    send_own(0)
+    for copy in locals_[:3]:
+        copy.wait()
+    slots = lax.broadcasted_iota(jnp.int32, (1, capacity), 1)
+    for to in range(peers):
+        idx_own[to, 0:1, :] = jnp.where(slots < count_smem[me, to], src_vmem[0, to : to + 1, :], -1)
+        idx_own[to, 1:2, :] = dst_vmem[to]
+    idx_in[me] = idx_own[me]
+
+    def send_idx(to):
+        remote(idx_own.at[to], idx_in.at[me], idx_send.at[0], idx_recv.at[me], to, core).start()
+
+    send_idx(other)
+    pl.when(has_up)(functools.partial(send_idx, up))
+    pl.when(has_down)(functools.partial(send_idx, down))
+    for c in range(1, CHUNKS - 1):
         send_own(c)
+    for copy in locals_[4:]:
+        copy.wait()
     par_copies = [
         remote(w_src_all.at[core], w_src_all.at[core], par_send.at[0], par_recv.at[0], me, mate),
         remote(bias_all.at[core], bias_all.at[core], par_send.at[1], par_recv.at[1], me, mate),
@@ -252,7 +275,7 @@
     pl.when(line == 0)(functools.partial(tell, 0, up))
     pl.when(line == lines - 1)(functools.partial(tell, 1, down))
 
-    def relays(part, send, z_recv, y_recv, late, arrived):
+    def relays(part, send, z_recv, y_recv, late, arrived, back=False):
         def extra(source, q, above):
             ref = part(source * 2 + 1 - side, q)
             remote(ref, ref, send.at[UP if above else DOWN], y_recv.at[source, q], up if above else down, core).start()
@@ -268,8 +291,10 @@
                     for at in range(lines)
                 ])
                 wanted = (source == line) & (to_giver == line)
-                if late(q):
-                    wanted = wanted | (to_end & (source == jnp.where(to < lines // 2, lines - 1, 0)))
+                if back:
+                    wanted = (source == line) & ((to_giver == line) | to_end) if late(q) else wanted
+                elif late(q):
+                    wanted = wanted | (to_end & (jnp.abs(source - to) > 1))
                 pl.when(there & wanted)(functools.partial(extra, source, q, above))
 
         def take_line(i, q, which):
@@ -285,13 +310,18 @@
                     ref = part(source * 2 + side, q)
                     remote(ref, ref, send.at[at], z_recv.at[source, q], me, mate).wait_recv()
 
+                    if back and lines > 2:
+                        to_line = line - 1 if above else line + 1
+                        onward = onward & ((to_line != (0 if above else lines - 1)) | (source != (lines - 1 if above else 0)))
+
                     @pl.when(onward)
                     def _():
                         remote(ref, ref, send.at[at], z_recv.at[source, q], to, core).start()
 
                     crossing = source != giver
                     if late(q):
-                        crossing = crossing & jnp.logical_not(end & (source == far))
+                        gap_of = jnp.abs(source - line)
+                        crossing = crossing & jnp.logical_not(end & ((gap_of == 1) if back else (gap_of > 1)))
 
                     @pl.when(crossing)
                     def _():
@@ -311,12 +341,12 @@
                 take(line)
                 return
             for source, valid in ((line + i, line + i < lines), (line - i, line - i >= 0)):
-                if late(q):
-                    valid = valid & jnp.logical_not(end & (source == far))
+                if late(q) and not back and i > 1:
+                    valid = valid & jnp.logical_not(end)
                 pl.when(valid)(functools.partial(take, source))
 
-        def take_far(q):
-            pl.when(end)(functools.partial(take_one, far, q))
+        def take_far(i, q):
+            pl.when(end)(functools.partial(take_one, jnp.where(low_half, line + i, line - i), q))
 
         def take_one(source, q):
             shard = source * 2 + 1 - side
@@ -335,13 +365,18 @@
     for i in range(lines - 1):
         source = by_line([nearest[at][i] for at in range(lines)])
         build_order += [source * 2 + side, source * 2 + 1 - side]
-    tables = [arrival_order(at, lines) for at in range(lines)]
-    order = []
-    for k in range(peers - 1):
-        source = by_line([tables[at][k][3] for at in range(lines)])
-        flip = by_line([tables[at][k][1] for at in range(lines)])
-        stage = max(tables[at][k][0] for at in range(lines))
-        order.append((stage, source * 2 + jnp.where(flip == 1, 1 - side, side)))
+
+    def by_stage(rule):
+        tables = [rule(at, lines) for at in range(lines)]
+        found = []
+        for k in range(peers - 1):
+            source = by_line([tables[at][k][3] for at in range(lines)])
+            flip = by_line([tables[at][k][1] for at in range(lines)])
+            stage = max(tables[at][k][0] for at in range(lines))
+            found.append((stage, source * 2 + jnp.where(flip == 1, 1 - side, side)))
+        return found
+
+    order, order_back = by_stage(arrival_order), by_stage(return_order)
 
     def build_enc(shard, wait=True):
         if wait:
@@ -415,8 +450,6 @@
     build_enc(me, wait=False)
     build_dec(me, wait=False)
     poll(1)
-    for c in range(CHUNKS // 2, CHUNKS - 1):
-        send_own(c)
     for copy in par_copies:
         copy.wait()
     w_src_all[...] = w_src_all[...] * 0.5
@@ -436,28 +469,34 @@
             tasks.pop(0)()
 
     def halves(c):
-        return c >= CHUNKS // 2
+        return c == CHUNKS - 1
 
     take_line, take_other, take_far = relays(x_part, x_send, xz_recv, xy_recv, halves, to_mate)
     def encodes(stage, parts):
         return [functools.partial(encode, shard, parts=parts) for at, shard in order if at == stage]
 
     run(2)
-    for i in range(lines):
+    for i in range(lines - 1):
         for c in range(CHUNKS):
-            if i < lines - 1:
-                take_line(i, c, None)
+            take_line(i, c, None)
             take_other(i, c)
             if i == lines - 2 and c == CHUNKS // 2:
-                tasks.append(dec_tasks.pop(0))
                 tasks += encodes(i, (0,))
-            if i == lines - 1 and c == CHUNKS // 2:
-                tasks += encodes(lines, (0,))
             run(1 + c // 2 if i == 0 else -(-len(tasks) // (CHUNKS - c)))
-        tasks += encodes(i, (1,) if i == lines - 2 else (0, 1))
-    for c in range(CHUNKS // 2, CHUNKS):
-        take_far(c)
-    run(len(tasks))
+        tasks += encodes(i, (0, 1) if i < lines - 2 else (1,))
+        if i == lines - 3:
+            tasks[1:1] = dec_tasks[:1]
+            tasks += dec_tasks[1:]
+            del dec_tasks[:]
+    tasks += encodes(lines, (0,))
+    for c in range(CHUNKS - 1):
+        take_other(lines - 1, c)
+        if c == CHUNKS - 2:
+            for gap in range(2, lines - 1):
+                take_far(gap, CHUNKS - 1)
+        run(-(-len(tasks) // (CHUNKS - 1 - c)))
+    if lines > 2:
+        take_far(lines - 1, CHUNKS - 1)
     for task in encodes(lines, (1,)):
         task()
 
@@ -497,9 +536,12 @@
         for flip in range(2):
             ref = proj_mate.at[pl.ds(sub * part_mesh, part_mesh)] if flip else into
             chan = mate if flip else core
-            for at, going, to, recv in (
-                (UP, has_up, up, pz_recv), (DOWN, has_down, down, pz_recv), (ACROSS, None, other, py_recv),
-            ):
+            routes = [(UP, has_up, up, pz_recv), (DOWN, has_down, down, pz_recv), (ACROSS, None, other, py_recv)]
+            if lines > 2:
+                routes[:0] = [
+                    (UP, line == 0, (lines - 1) * 2 + side, pz_recv), (DOWN, line == lines - 1, side, pz_recv),
+                ]
+            for at, going, to, recv in routes:
                 def go(ref=ref, into=into, at=at, to=to, recv=recv, q=2 * sub + flip, chan=chan):
                     remote(ref, into, p_send.at[at], recv.at[line, q], to, chan).start()
                 if going is None:
@@ -509,46 +551,62 @@
     whole_half = proj_all.at[pl.ds(my_first, half_mesh)]
     remote(proj_mate, whole_half, p_send.at[MATE], pm_recv.at[0], me, mate).start()
 
-    def decode(shard, first=False):
-        remote(dec.at[0, pl.ds(0, half_grid)], dec.at[0, pl.ds(0, half_grid)], dec_send.at[0], dec_recv.at[shard], me, mate).wait_recv()
-        rows = pl.ds(pl.multiple_of(shard * mesh_rows, mesh_rows), mesh_rows)
+    def decode(*shards):
+        some = dec.at[0, pl.ds(0, half_grid)]
+        for shard in shards:
+            remote(some, some, dec_send.at[0], dec_recv.at[shard], me, mate).wait_recv()
         for t in range(2):
             at = pl.ds(t * half_grid, half_grid)
-            acc[at, :] += jnp.dot(dec[shard, at, :], proj_all[rows, :], preferred_element_type=jnp.float32)
-
-    tasks = dec_tasks[:]
-    take_line, take_other, take_far = relays(
-        p_part, p_send, pz_recv, py_recv, lambda q: q >= SUBS, lambda shard, q: None)
+            acc[at, :] += sum(
+                jnp.dot(
+                    dec[shard, at, :], proj_all[pl.ds(pl.multiple_of(shard * mesh_rows, mesh_rows), mesh_rows), :],
+                    preferred_element_type=jnp.float32,
+                )
+                for shard in shards
+            )
+
+    take_line, take_other, _ = relays(
+        p_part, p_send, pz_recv, py_recv, lambda q: q >= SUBS, lambda shard, q: None, back=True)
     acc[...] = x_all[own_rows, pl.ds(pl.multiple_of(core * cols, cols), cols)].astype(jnp.float32)
 
     def own_decode():
         remote(proj_mate, whole_half, p_send.at[MATE], pm_recv.at[0], me, mate).wait_recv()
         decode(me)
 
-    tasks.append(flush)
     pieces = 2 * SUBS
-    while tasks:
-        tasks.pop(0)()
+    flush()
     tasks.append(own_decode)
-    for i in range(lines):
-        if i < lines - 1:
-            for q in range(pieces + 1):
-                if q < pieces:
-                    take_line(i, q, "inner")
-                if q:
-                    take_line(i, q - 1, "outer")
-        for q in range(pieces):
-            take_other(i, q)
-            if tasks and i:
-                tasks.pop(0)()
-        while tasks and i == 0:
-            tasks.pop(0)()
-        tasks.extend(functools.partial(decode, shard) for stage, shard in order if stage == i)
-    for q in range(SUBS, pieces):
-        take_far(q)
-    tasks.extend(functools.partial(decode, shard) for stage, shard in order if stage == lines)
-    while tasks:
-        tasks.pop(0)()
+
+    for q in range(pieces):
+        take_line(0, q, "inner")
+        if q:
+            take_other(0, q - 1)
+    take_other(0, pieces - 1)
+    for q in range(pieces):
+        take_line(0, q, "outer")
+    for q in range(pieces):
+        for i in range(1, lines - 1):
+            take_line(i, q, "inner")
+            take_line(i, q, "outer")
+        if q % 2:
+            run(1)
+    run(len(tasks))
+    early = [shard for at, shard in order_back if at < lines - 1]
+    for n in range(0, len(early), 2):
+        decode(*early[n : n + 2])
+    for q in range(pieces):
+        for i in range(1, lines):
+            if i > 1 or q < SUBS:
+                take_other(i, q)
+        if q == pieces - 2:
+            for late_q in range(SUBS, pieces):
+                take_other(1, late_q)
+            for at, shard in order_back:
+                if at == lines - 1:
+                    decode(shard)
+    final = [shard for at, shard in order_back if at >= lines]
+    if final:
+        decode(*final)
     out_ref[...] = acc[...].astype(jnp.bfloat16)
 
     def drained(ref, sem):
@@ -557,7 +615,7 @@
     for at in range(lines):
         @pl.when(line == at)
         def _(at=at):
-            for n, (x_n, p_n) in enumerate(zip(link_pieces(at, lines, CHUNKS), link_pieces(at, lines, pieces))):
+            for n, (x_n, p_n) in enumerate(zip(link_pieces(at, lines, CHUNKS), return_pieces(at, lines, pieces))):
                 if x_n:
                     drained(x_all.at[pl.ds(0, x_n * block)], x_send.at[n])
                     drained(proj_all.at[pl.ds(0, p_n * part_mesh)], p_send.at[n])

time: 49.9 us -> 48.7 us (0.976)
  Pallas kernels: 48.1 us -> 46.8 us
    pallas_call x1, Pallas kernels: 48.1 us -> 46.8 us  [fused(): pl.pallas_call(functools.partial(graph_kernel, peers), out_shape=jax.Shap...]
where the time goes in v3:
time: 48.7 us; the launch traced here: 48.5 us
  Pallas kernels  46.8 us (96%)
  local copies, waits for them, and re-layouts  1.67 us (3%)
    pallas_call x1, Pallas kernels, fused(): pl.pallas_call(functools.partial(graph_kernel, peers), out_shape=jax.Shap...  46.8 us
    unnamed x1, local copies, waits for them, and re-layouts  1.67 us

profile of v3, /device:TPU:0, one launch (start us, length us, event | category | flops | bytes accessed | tf_op | source)
XLA Modules:
  0.0 48.5 jit_solution(1304557681027772676)
XLA Ops:
  0.0 46.8 %shard_map.91 = bf16[1024,128]{1,0:T(8,128)(2,1)} custom-call(bf16[1024,256]{1,0:T(8,128)(2,1)} %x_ref.1, bf16[256,256]{1,0:T(8,128)(2,1)} %w_src_ref.1, f32[1,256]{1,0:T(1,128)} %bitcast.1, bf16[640,256]{1,0:T(8,128)(2,1)} %embed_ref.1, bf16[256,512]{1,0:T(8,128)(2,1)} %w_node_ref.1, bf16[256,256]{1,0:T(8,128)(2,1)} %w_dec_ref.1, s32[1,8,1024]{2,1,0:T(8,128)} %src_ref.1, ...), custom_call_target="tpu_custom_call" | custom-call | tf_op jit(solution)/shard_map/pallas_call | solution.py:638
  46.9 1.7 %copy.11 = bf16[1024,128]{1,0:T(8,128)(2,1)} copy(bf16[1024,128]{1,0:T(8,128)(2,1)} %shard_map.91) | data formatting | bytes 524288

commit v4 on v3

--- a/solution.py
+++ b/solution.py
@@ -10,6 +10,7 @@
 
 CHUNKS = 4
 SUBS = 2
+EARLY = 1
 HOT = jnp.float8_e4m3fn
 VMEM_BUDGET = 48 * 2**20
 MESH = pl.DeviceIdType.MESH
@@ -111,7 +112,8 @@
         gap = abs(source - line)
         if gap:
             split = is_end(line, lines) and gap > 1
-            stages += [(gap - 1, 0, gap, source), (lines if split else gap, 1, gap, source)]
+            shared = given(line, lines) is not None and gap == 1 and source != given(line, lines)
+            stages += [(gap - 1, 0, gap, source), (lines if split else 2 if shared else gap, 1, gap, source)]
     return sorted(stages)
 
 
@@ -119,13 +121,15 @@
     def extra(to):
         if not 0 <= to < lines:
             return 0
-        return lines - 2 if is_end(to, lines) else pieces if given(to, lines) == line else 0
+        if is_end(to, lines):
+            return lines - 2
+        return 0 if given(to, lines) is None else pieces if given(to, lines) == line else pieces // 2
 
     up = pieces * (line + 1) + extra(line + 1) if line < lines - 1 else 0
     down = pieces * (lines - line) + extra(line - 1) if line > 0 else 0
     across = pieces * lines
     if given(line, lines) is not None:
-        across -= pieces
+        across -= pieces + pieces // 2
     if is_end(line, lines):
         across -= lines - 2
     return up, down, across
@@ -147,12 +151,12 @@
         if not 0 <= to < lines:
             return 0
         onward = behind - (1 if direct and is_end(to, lines) and behind else 0)
-        beside = pieces // 2 if is_end(to, lines) else pieces if given(to, lines) == line else 0
+        beside = pieces - EARLY if is_end(to, lines) else pieces if given(to, lines) == line else 0
         return pieces * (1 + (1 if direct and first else 0) + onward) + beside
 
     up = one_way(line + 1, line, line == 0)
     down = one_way(line - 1, lines - 1 - line, line == lines - 1)
-    skipped = pieces if given(line, lines) is not None else pieces // 2 if is_end(line, lines) else 0
+    skipped = pieces if given(line, lines) is not None else pieces - EARLY if is_end(line, lines) else 0
     return up, down, pieces * lines - skipped
 
 
@@ -297,6 +301,14 @@
                     wanted = wanted | (to_end & (jnp.abs(source - to) > 1))
                 pl.when(there & wanted)(functools.partial(extra, source, q, above))
 
+        def extras_inner(q):
+            for above, there in ((True, has_up), (False, has_down)):
+                step = 1 if above else -1
+                wanted = by_line([
+                    1 if 0 <= at + step < lines and given(at + step, lines) not in (None, at) else 0 for at in range(lines)
+                ]) == 1
+                pl.when(there & wanted)(functools.partial(extra, line, q, above))
+
         def take_line(i, q, which):
             for above in (True, False):
                 source = line + 1 + i if above else line - 1 - i
@@ -319,6 +331,8 @@
                         remote(ref, ref, send.at[at], z_recv.at[source, q], to, core).start()
 
                     crossing = source != giver
+                    if not back and q >= CHUNKS // 2:
+                        crossing = crossing & ((giver < 0) | (jnp.abs(source - line) != 1))
                     if late(q):
                         gap_of = jnp.abs(source - line)
                         crossing = crossing & jnp.logical_not(end & ((gap_of == 1) if back else (gap_of > 1)))
@@ -343,28 +357,37 @@
             for source, valid in ((line + i, line + i < lines), (line - i, line - i >= 0)):
                 if late(q) and not back and i > 1:
                     valid = valid & jnp.logical_not(end)
+                if not back and q >= CHUNKS // 2 and i == 1:
+                    valid = valid & ((giver < 0) | (source == giver))
                 pl.when(valid)(functools.partial(take, source))
 
         def take_far(i, q):
             pl.when(end)(functools.partial(take_one, jnp.where(low_half, line + i, line - i), q))
 
-        def take_one(source, q):
+        def take_one(source, q, onward=False):
             shard = source * 2 + 1 - side
             ref = part(shard, q)
             remote(ref, ref, send.at[ACROSS], y_recv.at[source, q], me, mate).wait_recv()
+            if onward:
+                extras(source, q)
             arrived(shard, q)
 
-        return take_line, take_other, take_far
+        def take_shared(q):
+            source = jnp.where(low_half, line + 1, line - 1)
+            pl.when(giver >= 0)(functools.partial(take_one, source, q, onward=True))
+
+        return take_line, take_other, take_far, extras_inner, take_shared
 
     def to_mate(shard, c):
         ref = x_part(shard, c)
         remote(ref, ref, x_send.at[MATE], xm_recv.at[shard, c // (CHUNKS // 2)], me, mate).start()
 
     nearest = [sorted((p for p in range(lines) if p != at), key=lambda p: (abs(p - at), p)) for at in range(lines)]
+    sources = [by_line([nearest[at][i] for at in range(lines)]) for i in range(lines - 1)]
     build_order = [me, other]
-    for i in range(lines - 1):
-        source = by_line([nearest[at][i] for at in range(lines)])
-        build_order += [source * 2 + side, source * 2 + 1 - side]
+    for i in range(lines):
+        build_order += [source * 2 + side for source in sources[i : i + 1]]
+        build_order += [source * 2 + 1 - side for source in sources[max(i - 1, 0) : i]]
 
     def by_stage(rule):
         tables = [rule(at, lines) for at in range(lines)]
@@ -449,16 +472,13 @@
     poll(0)
     build_enc(me, wait=False)
     build_dec(me, wait=False)
-    poll(1)
     for copy in par_copies:
         copy.wait()
     w_src_all[...] = w_src_all[...] * 0.5
     bias_all[...] = bias_all[...] * 0.5
     encode(me, first=True)
-    for hop in range(2, lines - 1):
-        poll(hop)
-    for c in range(CHUNKS - 1, CHUNKS):
-        send_own(c)
+    poll(1)
+    send_own(CHUNKS - 1)
     enc_tasks = [functools.partial(build_enc, shard) for shard in build_order[1:]]
     dec_tasks = [functools.partial(build_dec, shard, wait=False) for shard in build_order[1:]]
     tasks = [task for pair in zip(enc_tasks[:-2], dec_tasks[:-2]) for task in pair] + enc_tasks[-2:]
@@ -471,23 +491,26 @@
     def halves(c):
         return c == CHUNKS - 1
 
-    take_line, take_other, take_far = relays(x_part, x_send, xz_recv, xy_recv, halves, to_mate)
+    take_line, take_other, take_far, extras_inner, take_shared = relays(x_part, x_send, xz_recv, xy_recv, halves, to_mate)
     def encodes(stage, parts):
         return [functools.partial(encode, shard, parts=parts) for at, shard in order if at == stage]
 
     run(2)
+    for hop in range(2, lines - 1):
+        poll(hop)
     for i in range(lines - 1):
         for c in range(CHUNKS):
             take_line(i, c, None)
             take_other(i, c)
+            if i == 2 and c < CHUNKS // 2:
+                take_shared(CHUNKS // 2 + c)
             if i == lines - 2 and c == CHUNKS // 2:
                 tasks += encodes(i, (0,))
             run(1 + c // 2 if i == 0 else -(-len(tasks) // (CHUNKS - c)))
+        if i == 0 and lines > 2:
+            for c in range(CHUNKS // 2, CHUNKS):
+                extras_inner(c)
         tasks += encodes(i, (0, 1) if i < lines - 2 else (1,))
-        if i == lines - 3:
-            tasks[1:1] = dec_tasks[:1]
-            tasks += dec_tasks[1:]
-            del dec_tasks[:]
     tasks += encodes(lines, (0,))
     for c in range(CHUNKS - 1):
         take_other(lines - 1, c)
@@ -565,8 +588,8 @@
                 for shard in shards
             )
 
-    take_line, take_other, _ = relays(
-        p_part, p_send, pz_recv, py_recv, lambda q: q >= SUBS, lambda shard, q: None, back=True)
+    take_line, take_other, *_ = relays(
+        p_part, p_send, pz_recv, py_recv, lambda q: q >= EARLY, lambda shard, q: None, back=True)
     acc[...] = x_all[own_rows, pl.ds(pl.multiple_of(core * cols, cols), cols)].astype(jnp.float32)
 
     def own_decode():
@@ -574,6 +597,8 @@
         decode(me)
 
     pieces = 2 * SUBS
+    tasks += dec_tasks
+    run(len(tasks))
     flush()
     tasks.append(own_decode)
 
@@ -596,10 +621,10 @@
         decode(*early[n : n + 2])
     for q in range(pieces):
         for i in range(1, lines):
-            if i > 1 or q < SUBS:
+            if i > 1 or q < EARLY:
                 take_other(i, q)
         if q == pieces - 2:
-            for late_q in range(SUBS, pieces):
+            for late_q in range(EARLY, pieces):
                 take_other(1, late_q)
             for at, shard in order_back:
                 if at == lines - 1:
@@ -679,7 +704,7 @@
     peers = lax.axis_size("graph")
     fits = (
         peers % 2 == 0
-        and peers >= 4
+        and peers in (4, 8)
         and lax.axis_size("chan") == 2
         and held_bytes(peers, grid_state, mesh_embed) <= VMEM_BUDGET
     )

time: 48.7 us -> 48.4 us (level)
  no operation moved by 1% of the time
where the time goes in v4:
time: 48.4 us; the launch traced here: 48.2 us
  Pallas kernels  46.5 us (96%)
  local copies, waits for them, and re-layouts  1.67 us (3%)
    pallas_call x1, Pallas kernels, fused(): pl.pallas_call(functools.partial(graph_kernel, peers), out_shape=jax.Shap...  46.5 us
    unnamed x1, local copies, waits for them, and re-layouts  1.67 us

profile of v4, /device:TPU:0, one launch (start us, length us, event | category | flops | bytes accessed | tf_op | source)
XLA Modules:
  0.0 48.2 jit_solution(16723050414260025225)
XLA Ops:
  0.0 46.5 %shard_map.91 = bf16[1024,128]{1,0:T(8,128)(2,1)} custom-call(bf16[1024,256]{1,0:T(8,128)(2,1)} %x_ref.1, bf16[256,256]{1,0:T(8,128)(2,1)} %w_src_ref.1, f32[1,256]{1,0:T(1,128)} %bitcast.1, bf16[640,256]{1,0:T(8,128)(2,1)} %embed_ref.1, bf16[256,512]{1,0:T(8,128)(2,1)} %w_node_ref.1, bf16[256,256]{1,0:T(8,128)(2,1)} %w_dec_ref.1, s32[1,8,1024]{2,1,0:T(8,128)} %src_ref.1, ...), custom_call_target="tpu_custom_call" | custom-call | tf_op jit(solution)/shard_map/pallas_call | solution.py:663
  46.5 1.7 %copy.11 = bf16[1024,128]{1,0:T(8,128)(2,1)} copy(bf16[1024,128]{1,0:T(8,128)(2,1)} %shard_map.91) | data formatting | bytes 524288

commit v5 on v4

--- a/solution.py
+++ b/solution.py
@@ -151,12 +151,12 @@
         if not 0 <= to < lines:
             return 0
         onward = behind - (1 if direct and is_end(to, lines) and behind else 0)
-        beside = pieces - EARLY if is_end(to, lines) else pieces if given(to, lines) == line else 0
+        beside = pieces - EARLY if direct and is_end(to, lines) else pieces if given(to, lines) == line else 0
         return pieces * (1 + (1 if direct and first else 0) + onward) + beside
 
     up = one_way(line + 1, line, line == 0)
     down = one_way(line - 1, lines - 1 - line, line == lines - 1)
-    skipped = pieces if given(line, lines) is not None else pieces - EARLY if is_end(line, lines) else 0
+    skipped = pieces if given(line, lines) is not None else pieces - EARLY if lines > 2 and is_end(line, lines) else 0
     return up, down, pieces * lines - skipped
 
 
@@ -295,10 +295,9 @@
                     for at in range(lines)
                 ])
                 wanted = (source == line) & (to_giver == line)
-                if back:
-                    wanted = (source == line) & ((to_giver == line) | to_end) if late(q) else wanted
-                elif late(q):
-                    wanted = wanted | (to_end & (jnp.abs(source - to) > 1))
+                if late(q):
+                    gap_to = jnp.abs(source - to)
+                    wanted = wanted | (to_end & ((gap_to == 2) if back else (gap_to > 1)))
                 pl.when(there & wanted)(functools.partial(extra, source, q, above))
 
         def extras_inner(q):
@@ -335,7 +334,7 @@
                         crossing = crossing & ((giver < 0) | (jnp.abs(source - line) != 1))
                     if late(q):
                         gap_of = jnp.abs(source - line)
-                        crossing = crossing & jnp.logical_not(end & ((gap_of == 1) if back else (gap_of > 1)))
+                        crossing = crossing & jnp.logical_not(end & ((gap_of == 2) if back else (gap_of > 1)))
 
                     @pl.when(crossing)
                     def _():
@@ -357,7 +356,7 @@
             for source, valid in ((line + i, line + i < lines), (line - i, line - i >= 0)):
                 if late(q) and not back and i > 1:
                     valid = valid & jnp.logical_not(end)
-                if not back and q >= CHUNKS // 2 and i == 1:
+                if i == 1 and (back or q >= CHUNKS // 2):
                     valid = valid & ((giver < 0) | (source == giver))
                 pl.when(valid)(functools.partial(take, source))
 
@@ -515,11 +514,9 @@
     for c in range(CHUNKS - 1):
         take_other(lines - 1, c)
         if c == CHUNKS - 2:
-            for gap in range(2, lines - 1):
+            for gap in range(2, lines):
                 take_far(gap, CHUNKS - 1)
         run(-(-len(tasks) // (CHUNKS - 1 - c)))
-    if lines > 2:
-        take_far(lines - 1, CHUNKS - 1)
     for task in encodes(lines, (1,)):
         task()
 
@@ -588,7 +585,7 @@
                 for shard in shards
             )
 
-    take_line, take_other, *_ = relays(
+    take_line, take_other, _, _, take_shared = relays(
         p_part, p_send, pz_recv, py_recv, lambda q: q >= EARLY, lambda shard, q: None, back=True)
     acc[...] = x_all[own_rows, pl.ds(pl.multiple_of(core * cols, cols), cols)].astype(jnp.float32)
 
@@ -607,6 +604,8 @@
         if q:
             take_other(0, q - 1)
     take_other(0, pieces - 1)
+    for q in range(pieces):
+        take_shared(q)
     for q in range(pieces):
         take_line(0, q, "outer")
     for q in range(pieces):
@@ -620,15 +619,13 @@
     for n in range(0, len(early), 2):
         decode(*early[n : n + 2])
     for q in range(pieces):
-        for i in range(1, lines):
-            if i > 1 or q < EARLY:
-                take_other(i, q)
-        if q == pieces - 2:
-            for late_q in range(EARLY, pieces):
-                take_other(1, late_q)
-            for at, shard in order_back:
-                if at == lines - 1:
-                    decode(shard)
+        take_other(1, q)
+    for at, shard in order_back:
+        if at == lines - 1:
+            decode(shard)
+    for q in range(pieces):
+        for i in range(2, lines):
+            take_other(i, q)
     final = [shard for at, shard in order_back if at >= lines]
     if final:
         decode(*final)

time: 48.4 us -> 46.9 us (0.969)
  Pallas kernels: 46.5 us -> 45 us
    pallas_call x1, Pallas kernels: 46.5 us -> 45 us  [fused(): pl.pallas_call(functools.partial(graph_kernel, peers), out_shape=jax.Shap...]
where the time goes in v5:
time: 46.9 us; the launch traced here: 46.7 us
  Pallas kernels  45 us (96%)
  local copies, waits for them, and re-layouts  1.67 us (4%)
    pallas_call x1, Pallas kernels, fused(): pl.pallas_call(functools.partial(graph_kernel, peers), out_shape=jax.Shap...  45 us
    unnamed x1, local copies, waits for them, and re-layouts  1.67 us

profile of v5, /device:TPU:0, one launch (start us, length us, event | category | flops | bytes accessed | tf_op | source)
XLA Modules:
  0.0 46.7 jit_solution(18224742123997908079)
XLA Ops:
  0.0 45.0 %shard_map.91 = bf16[1024,128]{1,0:T(8,128)(2,1)} custom-call(bf16[1024,256]{1,0:T(8,128)(2,1)} %x_ref.1, bf16[256,256]{1,0:T(8,128)(2,1)} %w_src_ref.1, f32[1,256]{1,0:T(1,128)} %bitcast.1, bf16[640,256]{1,0:T(8,128)(2,1)} %embed_ref.1, bf16[256,512]{1,0:T(8,128)(2,1)} %w_node_ref.1, bf16[256,256]{1,0:T(8,128)(2,1)} %w_dec_ref.1, s32[1,8,1024]{2,1,0:T(8,128)} %src_ref.1, ...), custom_call_target="tpu_custom_call" | custom-call | tf_op jit(solution)/shard_map/pallas_call | solution.py:660
  45.0 1.7 %copy.11 = bf16[1024,128]{1,0:T(8,128)(2,1)} copy(bf16[1024,128]{1,0:T(8,128)(2,1)} %shard_map.91) | data formatting | bytes 524288

commit v6 on v5

--- a/solution.py
+++ b/solution.py
@@ -160,15 +160,24 @@
     return up, down, pieces * lines - skipped
 
 
+class Shifted:
+    def __init__(self, ref, first):
+        self.ref, self.first, self.at = ref, first, self
+
+    def __getitem__(self, index):
+        return self.ref.at[self.first + index]
+
+
 def graph_kernel(
     peers,
     x_ref, w_src_ref, bias_ref, embed_ref, w_node_ref, w_dec_ref, src_ref, dst_ref, count_ref,
     out_ref,
     x_all, idx_own, idx_in, src_vmem, dst_vmem, count_smem, w_src_all, bias_all, embed_all, w_node_all, w_dec_all,
-    enc, dec, hot, msg, agg, acc, proj_mate, proj_all,
-    ready, local_sem, par_send, par_recv, idx_send, idx_recv,
-    x_send, xz_recv, xy_recv, xm_recv, p_send, pz_recv, py_recv, pm_recv, dec_send, dec_recv,
+    enc, dec, hot, msg, agg, acc, out_vmem, proj_mate, proj_all,
+    ready, local_sem, par_recv, idx_send, idx_recv,
+    x_send, xz_recv, xy_recv, xm_recv, pz_recv, py_recv, pm_recv, dec_send, dec_recv,
 ):
+    par_send = p_send = Shifted(local_sem, 4)
     lines = peers // 2
     me = lax.axis_index("graph")
     core = lax.axis_index("chan")
@@ -571,19 +580,25 @@
     whole_half = proj_all.at[pl.ds(my_first, half_mesh)]
     remote(proj_mate, whole_half, p_send.at[MATE], pm_recv.at[0], me, mate).start()
 
-    def decode(*shards):
+    def arrived_dec(*shards):
         some = dec.at[0, pl.ds(0, half_grid)]
         for shard in shards:
             remote(some, some, dec_send.at[0], dec_recv.at[shard], me, mate).wait_recv()
+
+    def products(at, shards):
+        return sum(
+            jnp.dot(
+                dec[shard, at, :], proj_all[pl.ds(pl.multiple_of(shard * mesh_rows, mesh_rows), mesh_rows), :],
+                preferred_element_type=jnp.float32,
+            )
+            for shard in shards
+        )
+
+    def decode(*shards):
+        arrived_dec(*shards)
         for t in range(2):
             at = pl.ds(t * half_grid, half_grid)
-            acc[at, :] += sum(
-                jnp.dot(
-                    dec[shard, at, :], proj_all[pl.ds(pl.multiple_of(shard * mesh_rows, mesh_rows), mesh_rows), :],
-                    preferred_element_type=jnp.float32,
-                )
-                for shard in shards
-            )
+            acc[at, :] += products(at, shards)
 
     take_line, take_other, _, _, take_shared = relays(
         p_part, p_send, pz_recv, py_recv, lambda q: q >= EARLY, lambda shard, q: None, back=True)
@@ -627,9 +642,13 @@
         for i in range(2, lines):
             take_other(i, q)
     final = [shard for at, shard in order_back if at >= lines]
-    if final:
-        decode(*final)
-    out_ref[...] = acc[...].astype(jnp.bfloat16)
+    arrived_dec(*final)
+    outs = []
+    for t in range(2):
+        at = pl.ds(t * half_grid, half_grid)
+        out_vmem[at, :] = (acc[at, :] + products(at, final)).astype(jnp.bfloat16)
+        outs.append(pltpu.make_async_copy(out_vmem.at[at], out_ref.at[at], local_sem.at[t]))
+        outs[t].start()
 
     def drained(ref, sem):
         remote(ref, ref, sem, sem, me, mate).wait_send()
@@ -645,6 +664,8 @@
     drained(proj_mate, p_send.at[MATE])
     drained(idx_own.at[pl.ds(0, peers - 1)], idx_send.at[0])
     drained(dec.at[:, pl.ds(0, half_grid)], dec_send.at[0])
+    for copy in outs:
+        copy.wait()
 
 
 def fused(grid_state, w_src, bias_src, mesh_embed, w_node, w_dec, slot_src, slot_dst, slot_count):
@@ -661,7 +682,7 @@
         functools.partial(graph_kernel, peers),
         out_shape=jax.ShapeDtypeStruct((grid_rows, chans // 2), bf16),
         in_specs=[pl.BlockSpec(memory_space=pl.ANY)] * 9,
-        out_specs=pl.BlockSpec(memory_space=pltpu.VMEM),
+        out_specs=pl.BlockSpec(memory_space=pl.ANY),
         scratch_shapes=[
             pltpu.VMEM((peers * grid_rows, chans), bf16),
             pltpu.VMEM((peers, 2, capacity), i32),
@@ -680,12 +701,13 @@
             pltpu.VMEM((grid_rows, 2 * hidden), bf16),
             pltpu.VMEM((mesh_rows // 2, 2 * hidden), f32),
             pltpu.VMEM((grid_rows, chans // 2), f32),
+            pltpu.VMEM((grid_rows, chans // 2), bf16),
             pltpu.VMEM((mesh_rows // 2, chans // 2), bf16),
             pltpu.VMEM((peers * mesh_rows, chans // 2), bf16),
             pltpu.SemaphoreType.REGULAR((2,)),
-            dma((9,)), dma((5,)), dma((5,)), dma((1,)), dma((peers,)),
+            dma((9,)), dma((5,)), dma((1,)), dma((peers,)),
             dma((4,)), dma((lines, CHUNKS)), dma((lines, CHUNKS)), dma((peers, 2)),
-            dma((4,)), dma((lines, pieces)), dma((lines, pieces)), dma((1,)), dma((1,)), dma((peers,)),
+            dma((lines, pieces)), dma((lines, pieces)), dma((1,)), dma((1,)), dma((peers,)),
         ],
         compiler_params=pltpu.CompilerParams(collective_id=0, has_side_effects=True),
     )(grid_state, w_src, bias_src[None, :], mesh_embed, w_node, w_dec, slot_src, slot_dst, slot_count)
@@ -700,8 +722,7 @@
 def per_device(grid_state, w_src, bias_src, mesh_embed, *rest):
     peers = lax.axis_size("graph")
     fits = (
-        peers % 2 == 0
-        and peers in (4, 8)
+        peers == 2 * CHUNKS
         and lax.axis_size("chan") == 2
         and held_bytes(peers, grid_state, mesh_embed) <= VMEM_BUDGET
     )

time: 46.9 us -> 46.7 us (level)
  no operation moved by 1% of the time
where the time goes in v6:
time: 46.7 us; the launch traced here: 46.5 us
  Pallas kernels  44.9 us (96%)
  local copies, waits for them, and re-layouts  1.67 us (4%)
    pallas_call x1, Pallas kernels, fused(): pl.pallas_call(functools.partial(graph_kernel, peers), out_shape=jax.Shap...  44.9 us
    unnamed x1, local copies, waits for them, and re-layouts  1.67 us

profile of v6, /device:TPU:0, one launch (start us, length us, event | category | flops | bytes accessed | tf_op | source)
XLA Modules:
  0.0 46.5 jit_solution(15926771941117286673)
XLA Ops:
  0.0 44.9 %shard_map.91 = bf16[1024,128]{1,0:T(8,128)(2,1)} custom-call(bf16[1024,256]{1,0:T(8,128)(2,1)} %x_ref.1, bf16[256,256]{1,0:T(8,128)(2,1)} %w_src_ref.1, f32[1,256]{1,0:T(1,128)} %bitcast.1, bf16[640,256]{1,0:T(8,128)(2,1)} %embed_ref.1, bf16[256,512]{1,0:T(8,128)(2,1)} %w_node_ref.1, bf16[256,256]{1,0:T(8,128)(2,1)} %w_dec_ref.1, s32[1,8,1024]{2,1,0:T(8,128)} %src_ref.1, ...), custom_call_target="tpu_custom_call" | custom-call | tf_op jit(solution)/shard_map/pallas_call | solution.py:681
  44.9 1.7 %copy.11 = bf16[1024,128]{1,0:T(8,128)(2,1)} copy(bf16[1024,128]{1,0:T(8,128)(2,1)} %shard_map.91) | data formatting | bytes 524288
